TPU v7x, 32 devices: a whole 2x2x4 slice. The times are simulated.
32 devices in a mesh: dp: 2 (over x), ep: 16 (over z, y, core).
Axes of the slice: x: 2, y: 2, z: 4, core: 2. Of those that a mesh axis runs over, the one named last changes fastest.
Arguments:
- hidden_state: bfloat16 [4096, 1024], P(('dp', 'ep')), parts along dimension 0
- key_cache: bfloat16 [2, 4096, 32, 8, 64], P(None, ('dp', 'ep')), parts along dimension 1
- value_cache: bfloat16 [2, 4096, 32, 8, 64], P(None, ('dp', 'ep')), parts along dimension 1
- positions: int32 [4096], P(('dp', 'ep')), parts along dimension 0
- expert_ids: int32 [2, 4096, 8], P(None, ('dp', 'ep')), parts along dimension 1
- attn_gain: float32 [2, 1024], replicated
- w_query: bfloat16 [2, 1024, 1024], replicated
- w_key: bfloat16 [2, 1024, 512], replicated
- w_value: bfloat16 [2, 1024, 512], replicated
- q_gain: float32 [2, 1024], replicated
- k_gain: float32 [2, 512], replicated
- w_out: bfloat16 [2, 1024, 1024], replicated
- moe_gain: float32 [2, 1024], replicated
- w_router: bfloat16 [2, 1024, 32], replicated
- w_gate: bfloat16 [2, 32, 1024, 512], P(None, 'ep')
- w_up: bfloat16 [2, 32, 1024, 512], P(None, 'ep')
- w_down: bfloat16 [2, 32, 512, 1024], P(None, 'ep')
Outputs:
- output 1: bfloat16 [4096, 1024], P(('dp', 'ep')), parts along dimension 0
- output 2: bfloat16 [2, 4096, 32, 8, 64], P(None, ('dp', 'ep')), parts along dimension 1
- output 3: bfloat16 [2, 4096, 32, 8, 64], P(None, ('dp', 'ep')), parts along dimension 1
There are 2 independent parts. A program takes and returns all parts, laid end to end along the dimension named above; an argument that names none is the same for every part.
All inputs are finite; a program needn't handle non-finite values.
Results may differ from a plain program's by a relative error of at most 0.0191773.
Values are sent between devices in bfloat16 or wider.
A program may use at most 1 GiB of HBM per device.

v0:
```python
import jax
import jax.numpy as jnp
from jax import lax
from jax.sharding import PartitionSpec as P

NORM_EPS = 1e-5
ROPE_THETA = 10000.0


def rms_scale(tensor, gain):
    mean_sq = jnp.mean(tensor * tensor, axis=-1, keepdims=True)
    return tensor * lax.rsqrt(mean_sq + NORM_EPS) * gain


def rotate_heads(tensor, positions):
    head_dim = tensor.shape[-1]
    half_dim = head_dim // 2
    inv_freq = ROPE_THETA ** (-jnp.arange(0, head_dim, 2, dtype=jnp.float32) / head_dim)
    angles = positions.astype(jnp.float32)[:, None] * inv_freq[None, :]
    angles = jnp.concatenate([angles, angles], axis=-1)[:, None, :]
    turned = jnp.concatenate([-tensor[..., half_dim:], tensor[..., :half_dim]], axis=-1)
    return tensor * jnp.cos(angles) + turned * jnp.sin(angles)


def attention_layer(hidden_x, key_l, value_l, positions, attn_gain, w_query, w_key, w_value, q_gain, k_gain, w_out):
    batch_rows, num_slots, kv_heads, head_dim = key_l.shape
    num_heads = w_query.shape[1] // head_dim
    normed = rms_scale(hidden_x.astype(jnp.float32), attn_gain).astype(jnp.bfloat16)
    query_rot = rms_scale(jnp.dot(normed, w_query, preferred_element_type=jnp.float32), q_gain)
    query_rot = rotate_heads(query_rot.reshape(batch_rows, num_heads, head_dim), positions).astype(jnp.bfloat16)
    key_new = rms_scale(jnp.dot(normed, w_key, preferred_element_type=jnp.float32), k_gain)
    key_new = rotate_heads(key_new.reshape(batch_rows, kv_heads, head_dim), positions).astype(jnp.bfloat16)
    value_new = jnp.dot(normed, w_value, preferred_element_type=jnp.float32).astype(jnp.bfloat16).reshape(batch_rows, kv_heads, head_dim)
    slot_ids = jnp.arange(num_slots)
    at_pos = (slot_ids[None, :] == positions[:, None])[:, :, None, None]
    key_l = jnp.where(at_pos, key_new[:, None], key_l)
    value_l = jnp.where(at_pos, value_new[:, None], value_l)
    grouped = query_rot.reshape(batch_rows, kv_heads, num_heads // kv_heads, head_dim)
    scores = jnp.einsum('bkgh,bskh->bkgs', grouped, key_l, preferred_element_type=jnp.float32) * head_dim ** -0.5
    visible = (slot_ids[None, :] <= positions[:, None])[:, None, None, :]
    attn_probs = jax.nn.softmax(jnp.where(visible, scores, -jnp.inf), axis=-1).astype(jnp.bfloat16)
    attended = jnp.einsum('bkgs,bskh->bkgh', attn_probs, value_l, preferred_element_type=jnp.float32).astype(jnp.bfloat16)
    attn_out = jnp.dot(attended.reshape(batch_rows, num_heads * head_dim), w_out, preferred_element_type=jnp.float32)
    return (hidden_x.astype(jnp.float32) + attn_out).astype(jnp.bfloat16), key_l, value_l


def route_tables(choice_ids, experts, capacity):
    batch_loc = choice_ids.shape[0]
    member = jnp.sum((choice_ids[:, :, None] == jnp.arange(experts)).astype(jnp.int32), axis=1)
    slot_of = jnp.cumsum(member, axis=0) - member
    filled = (slot_of.T[:, :, None] == jnp.arange(capacity)) & (member.T[:, :, None] > 0)
    seq_ids = jnp.arange(batch_loc)[None, :, None]
    token_of = jnp.sum(jnp.where(filled, seq_ids, 0), axis=1) + batch_loc * (1 - jnp.any(filled, axis=1).astype(jnp.int32))
    choice_slot = jnp.take_along_axis(slot_of, choice_ids, axis=1)
    return token_of, choice_slot


def moe_layer(hidden_x, choice_ids, moe_gain, w_router, w_gate, w_up, w_down, group_size):
    batch_loc, top_k = choice_ids.shape
    local_experts, hidden_dim = w_gate.shape[0], w_gate.shape[1]
    experts = local_experts * group_size
    capacity = (4 * batch_loc * top_k + experts - 1) // experts
    normed = rms_scale(hidden_x.astype(jnp.float32), moe_gain).astype(jnp.bfloat16)
    probs = jax.nn.softmax(jnp.dot(normed, w_router, preferred_element_type=jnp.float32), axis=-1)
    gate_vals = jnp.take_along_axis(probs, choice_ids, axis=1)
    token_of, choice_slot = route_tables(choice_ids, experts, capacity)
    send_index = token_of.reshape(group_size, local_experts, capacity).transpose(1, 0, 2)
    send_rows = jnp.take(normed, send_index, axis=0, mode='fill', fill_value=0)
    received = lax.all_to_all(send_rows, 'ep', 1, 1, tiled=True)
    gate_part = jnp.einsum('escd,edf->escf', received, w_gate, preferred_element_type=jnp.float32)
    up_part = jnp.einsum('escd,edf->escf', received, w_up, preferred_element_type=jnp.float32)
    activated = (jax.nn.silu(gate_part) * up_part).astype(jnp.bfloat16)
    expert_out = jnp.einsum('escf,efd->escd', activated, w_down, preferred_element_type=jnp.float32).astype(jnp.bfloat16)
    returned = lax.all_to_all(expert_out, 'ep', 1, 1, tiled=True)
    flat_index = ((choice_ids % local_experts) * group_size + choice_ids // local_experts) * capacity + choice_slot
    picked = jnp.take(returned.reshape(experts * capacity, hidden_dim), flat_index, axis=0)
    mixed_sum = jnp.sum(gate_vals[:, :, None] * picked.astype(jnp.float32), axis=1)
    return (hidden_x.astype(jnp.float32) + mixed_sum).astype(jnp.bfloat16)


def solution(mesh):
    group_size = mesh.shape['ep']
    seq_axes = ('dp', 'ep')

    def device_step(hidden_state, key_cache, value_cache, positions, expert_ids, attn_gain, w_query, w_key, w_value, q_gain, k_gain, w_out, moe_gain, w_router, w_gate, w_up, w_down):
        hidden_x = hidden_state
        new_keys = []
        new_values = []
        for layer_idx in range(key_cache.shape[0]):
            hidden_x, key_l, value_l = attention_layer(hidden_x, key_cache[layer_idx], value_cache[layer_idx], positions, attn_gain[layer_idx], w_query[layer_idx], w_key[layer_idx], w_value[layer_idx], q_gain[layer_idx], k_gain[layer_idx], w_out[layer_idx])
            new_keys.append(key_l)
            new_values.append(value_l)
            hidden_x = moe_layer(hidden_x, expert_ids[layer_idx], moe_gain[layer_idx], w_router[layer_idx], w_gate[layer_idx], w_up[layer_idx], w_down[layer_idx], group_size)
        return hidden_x, jnp.stack(new_keys), jnp.stack(new_values)

    cache_spec = P(None, seq_axes, None, None, None)
    expert_spec = P(None, 'ep', None, None)
    in_specs = (P(seq_axes, None), cache_spec, cache_spec, P(seq_axes), P(None, seq_axes, None)) + (P(),) * 9 + (expert_spec,) * 3
    out_specs = (P(seq_axes, None), cache_spec, cache_spec)
    return jax.shard_map(device_step, mesh=mesh, in_specs=in_specs, out_specs=out_specs, check_vma=False)
```

profile of v0, /device:TPU:15, one launch (start us, length us, event | category | flops | bytes accessed | tf_op | source)
XLA Modules:
  0.0 1030.3 jit_solution(10144497502415264843)
XLA Ops:
  26.1 12.9 %copy.179 = bf16[128,32,8,64]{3,1,2,0:T(8,128)(2,1)} copy(bf16[128,32,8,64]{0,3,2,1:T(8,128)(2,1)} %get-tuple-element.45) | data formatting | bytes 8388608 | tf_op jit(solution)/shard_map/jit(_where)/select_n | solution.py:36
  39.0 12.9 %copy.181 = bf16[128,32,8,64]{3,1,2,0:T(8,128)(2,1)} copy(bf16[128,32,8,64]{0,3,2,1:T(8,128)(2,1)} %get-tuple-element.46) | data formatting | bytes 8388608 | tf_op jit(solution)/shard_map/jit(_where)/select_n | solution.py:37
  52.0 7.9 fusion.142
  68.7 18.1 %gather_fusion.1 = bf16[4096,1024]{1,0:T(8,128)(2,1)} fusion(bf16[128,1024]{1,0:T(8,128)(2,1)S(1)} %multiply_convert_fusion.5, s32[4096]{0:T(1024)S(1)} %broadcast_clamp_fusion.1), kind=kCustom, calls=%fused_computation.1.clone | custom fusion | bytes 16793600 | tf_op jit(solution)/shard_map/jit(_take)/gather | solution.py:68
  91.3 188.6 %all_to_all.20 = bf16[2,16,128,1024]{3,2,0,1:T(8,128)(2,1)S(1)} all-to-all(bf16[2,16,128,1024]{3,2,0,1:T(8,128)(2,1)S(1)} %copy_select_fusion.1), channel_id=1, replica_groups=mesh['dp'=2,'ep'=16] {'ep'}, dimensions={1} | all-to-all | bytes 16777216 | tf_op jit(solution)/shard_map/all_to_all | solution.py:69
  290.0 16.4 %convolution_convert_fusion.1 = bf16[2,16,128,1024]{3,2,1,0:T(8,128)(2,1)} fusion(f32[2,16,128,512]{3,2,1,0:T(8,128)} %fusion.6, bf16[2,16,128,1024]{3,2,0,1:T(8,128)(2,1)} %copy-done, bf16[2,2,512,1024]{3,2,1,0:T(8,128)(2,1)} %param.41, bf16[2,2,1024,512]{3,2,1,0:T(8,128)(2,1)} %param.39), kind=kOutput, calls=%fused_computation.25 | convolution fusion | flops 8606711808 | bytes 29360128 | tf_op jit(solution)/shard_map/escf,efd->escd/dot_general | solution.py:73
  306.4 8.4 copy.196
  321.4 7.1 gather_fusion.6
  331.8 7.1 gather_fusion.2
  347.0 156.4 %all-to-all-done.1 = bf16[2,16,128,1024]{3,2,0,1:T(8,128)(2,1)} async-done(((bf16[2,16,128,1024]{3,2,0,1:T(8,128)(2,1)}), bf16[2,16,128,1024]{3,2,0,1:T(8,128)(2,1)}, u32[]{:S(2)}, u32[]{:S(2)}) %all-to-all-start.1) | async-done | bytes 8388640 | tf_op jit(solution)/shard_map/all_to_all | solution.py:74
  503.3 8.4 copy.197
  511.7 9.4 gather_fusion.3
  534.2 12.9 %copy.203 = bf16[128,32,8,64]{3,1,2,0:T(8,128)(2,1)} copy(bf16[128,32,8,64]{0,3,2,1:T(8,128)(2,1)} %get-tuple-element.41) | data formatting | bytes 8388608 | tf_op jit(solution)/shard_map/jit(_where)/select_n | solution.py:36
  547.2 12.9 %copy.205 = bf16[128,32,8,64]{3,1,2,0:T(8,128)(2,1)} copy(bf16[128,32,8,64]{0,3,2,1:T(8,128)(2,1)} %get-tuple-element.42) | data formatting | bytes 8388608 | tf_op jit(solution)/shard_map/jit(_where)/select_n | solution.py:37
  560.1 8.1 fusion.144
  577.1 18.1 %gather_fusion.5 = bf16[4096,1024]{1,0:T(8,128)(2,1)} fusion(bf16[128,1024]{1,0:T(8,128)(2,1)S(1)} %multiply_convert_fusion.4, s32[4096]{0:T(1024)S(1)} %broadcast_clamp_fusion), kind=kCustom, calls=%fused_computation.5.clone | custom fusion | bytes 16793600 | tf_op jit(solution)/shard_map/jit(_take)/gather | solution.py:68
  599.7 187.0 %all_to_all.21 = bf16[2,16,128,1024]{3,2,0,1:T(8,128)(2,1)S(1)} all-to-all(bf16[2,16,128,1024]{3,2,0,1:T(8,128)(2,1)S(1)} %copy_select_fusion), channel_id=1, replica_groups=mesh['dp'=2,'ep'=16] {'ep'}, dimensions={1} | all-to-all | bytes 16777216 | tf_op jit(solution)/shard_map/all_to_all | solution.py:69
  796.8 16.4 %convolution_convert_fusion = bf16[2,16,128,1024]{3,2,1,0:T(8,128)(2,1)} fusion(f32[2,16,128,512]{3,2,1,0:T(8,128)} %fusion.2, bf16[2,16,128,1024]{3,2,0,1:T(8,128)(2,1)} %copy-done.1, bf16[2,2,512,1024]{3,2,1,0:T(8,128)(2,1)} %param.41, bf16[2,2,1024,512]{3,2,1,0:T(8,128)(2,1)} %param.39), kind=kOutput, calls=%fused_computation.24 | convolution fusion | flops 8606711808 | bytes 29360128 | tf_op jit(solution)/shard_map/escf,efd->escd/dot_general | solution.py:73
  813.1 8.2 copy.220
  835.4 10.6 %broadcast_select_fusion.1 = (bf16[1,128,32,8,64]{1,4,3,2,0:T(8,128)(2,1)}, bf16[1,128,32,8,64]{1,4,3,2,0:T(8,128)(2,1)}, bf16[1,128,32,8,64]{1,4,3,2,0:T(8,128)(2,1)S(1)}, bf16[1,128,32,8,64]{1,4,3,2,0:T(8,128)(2,1)}) fusion(pred[128,32]{0,1:T(8,128)(4,1)S(1)} %copy-done.14, bf16[2,128,32,8,64]{1,4,3,2,0:T(8,128)(2,1)} %param.27, ...), kind=kLoop, calls=%fused_computation.35 | loop fusion | flops 8388608 | bytes 34082816 | tf_op jit(solution)/shard_map/jit(_where)/select_n | solution.py:37
  845.9 7.6 pad_maximum_fusion.1
  859.9 150.0 %all-to-all-done.3 = bf16[2,16,128,1024]{3,2,0,1:T(8,128)(2,1)} async-done(((bf16[2,16,128,1024]{3,2,0,1:T(8,128)(2,1)}), bf16[2,16,128,1024]{3,2,0,1:T(8,128)(2,1)}, u32[]{:S(2)}, u32[]{:S(2)}) %all-to-all-start.3) | async-done | bytes 8388640 | tf_op jit(solution)/shard_map/all_to_all | solution.py:74
  1009.9 8.2 copy.221
  1018.1 9.4 gather_fusion.7
  (174 shorter events, 125.4 us)
Async XLA Ops:
  0.6 16.1 %copy-start.6 = (bf16[128,1024]{1,0:T(8,128)(2,1)S(1)}, bf16[128,1024]{1,0:T(8,128)(2,1)}, u32[]{:S(2)}) copy-start(bf16[128,1024]{1,0:T(8,128)(2,1)} %param.25) | copy-start | bytes 786436
  2.0 18.0 %copy-start.13 = (pred[128,32]{0,1:T(8,128)(4,1)}, pred[128,32]{0,1:T(8,128)(4,1)S(1)}, u32[]{:S(2)}) copy-start(pred[128,32]{0,1:T(8,128)(4,1)S(1)} %get-tuple-element.48) | copy-start | bytes 12292
  12.7 39.3 %copy-start.17 = (pred[128,32]{1,0:T(8,128)(4,1)}, pred[128,32]{1,0:T(8,128)(4,1)S(1)}, u32[]{:S(2)}) copy-start(pred[128,32]{1,0:T(8,128)(4,1)S(1)} %copy.174) | copy-start | bytes 12292
  12.9 7.1 copy-start.7
  12.9 7.1 copy-start.9
  14.7 5.3 copy-start.2
  20.0 6.1 copy-start.4
  91.3 192.0 %copy-start.22 = (bf16[2,2,1024,512]{3,2,1,0:T(8,128)(2,1)S(1)}, bf16[2,2,1024,512]{3,2,1,0:T(8,128)(2,1)}, u32[]{:S(2)}) copy-start(bf16[2,2,1024,512]{3,2,1,0:T(8,128)(2,1)} %param.40) | copy-start | bytes 12582916
  279.9 3.4 copy-start
  314.8 6.2 copy-start.11
  314.8 188.6 %all-to-all-start.1 = ((bf16[2,16,128,1024]{3,2,0,1:T(8,128)(2,1)}), bf16[2,16,128,1024]{3,2,0,1:T(8,128)(2,1)}, u32[]{:S(2)}, u32[]{:S(2)}) async-start(bf16[2,16,128,1024]{3,2,0,1:T(8,128)(2,1)} %copy.196), calls=%async_computation.1 | async-start | bytes 16777216 | tf_op jit(solution)/shard_map/all_to_all | solution.py:74
  331.7 7.6 copy-start.12
  511.7 11.1 %copy-start.20 = (f32[1,1024]{1,0:T(1,128)S(1)}, f32[1,1024]{1,0:T(1,128)}, u32[]{:S(2)}) copy-start(f32[1,1024]{1,0:T(1,128)} %get-tuple-element.37) | copy-start | bytes 12292
  521.2 5.0 copy-start.21
  522.8 4.0 copy-start.19
  522.9 4.3 copy-start.16
  526.7 1.5 copy-start.14
  547.2 13.0 %copy-start.18 = (pred[128,32]{1,0:T(8,128)(4,1)S(1)}, pred[128,32]{1,0:T(8,128)(4,1)}, u32[]{:S(2)}) copy-start(pred[128,32]{1,0:T(8,128)(4,1)} %copy-done.17) | copy-start | bytes 12292
  568.2 8.8 copy-start.15
  599.7 190.4 %copy-start.23 = (bf16[2,2,1024,512]{3,2,1,0:T(8,128)(2,1)S(1)}, bf16[2,2,1024,512]{3,2,1,0:T(8,128)(2,1)}, u32[]{:S(2)}) copy-start(bf16[2,2,1024,512]{3,2,1,0:T(8,128)(2,1)} %param.40) | copy-start | bytes 12582916
  786.6 3.4 copy-start.1
  821.3 188.6 %all-to-all-start.3 = ((bf16[2,16,128,1024]{3,2,0,1:T(8,128)(2,1)}), bf16[2,16,128,1024]{3,2,0,1:T(8,128)(2,1)}, u32[]{:S(2)}, u32[]{:S(2)}) async-start(bf16[2,16,128,1024]{3,2,0,1:T(8,128)(2,1)} %copy.220), calls=%async_computation.3 | async-start | bytes 16777216 | tf_op jit(solution)/shard_map/all_to_all | solution.py:74
  828.0 7.3 copy-start.3
  828.0 7.3 copy-start.5
  (2 other events, 2.8 us)
where the time goes:
time: 1040 us; the launch traced here: 1030 us
  blocking collectives  376 us (36%)
  waiting for transfers between devices  306 us (29%)
  local copies, waits for them, and re-layouts  186 us (18%)
  matrix products  88.5 us (9%)
  other arithmetic  59.5 us (6%)
  starting transfers between devices  12.2 us (1%)
    all_to_all x2, blocking collectives, moe_layer(): received = lax.all_to_all(send_rows, 'ep', 1, 1, tiled=True)  376 us
    all_to_all x2, waiting for transfers between devices, moe_layer(): returned = lax.all_to_all(expert_out, 'ep', 1, 1, tiled=True)  306 us
    gather x2, local copies, waits for them, and re-layouts, moe_layer(): send_rows = jnp.take(normed, send_index, axis=0, mode='fill', fill_value=0)  36.3 us
    dot_general x2, matrix products, moe_layer(): jnp.einsum('escf,efd->escd', activated, w_down, preferred_element_type=jn...  32.7 us
    select_n x2, local copies, waits for them, and re-layouts, attention_layer(): value_l = jnp.where(at_pos, value_new[:, None], value_l)  25.9 us
    select_n x2, local copies, waits for them, and re-layouts, attention_layer(): key_l = jnp.where(at_pos, key_new[:, None], key_l)  25.9 us
  transfers between devices with their start and end apart: 2, of which 2 were waited for; matrix products, arithmetic and copies ran while one was open for 6% of the time, Pallas kernels for 0%

commit v1 on v0

v1 whole, which is shorter than its diff:
```python
import functools

import jax
import jax.numpy as jnp
from jax import lax
from jax.experimental import pallas as pl
from jax.experimental.pallas import tpu as pltpu
from jax.sharding import PartitionSpec as P

NORM_EPS = 1e-5
ROPE_THETA = 10000.0
F32 = jnp.float32
BF16 = jnp.bfloat16
MESH = pl.DeviceIdType.MESH
RS_SUBS = 4
AG_SUBS = 2
VMEM_LIMIT = 60 * 1024 * 1024


def rms_scale(tensor, gain):
    mean_sq = jnp.mean(tensor * tensor, axis=-1, keepdims=True)
    return tensor * lax.rsqrt(mean_sq + NORM_EPS) * gain


def attention_kernel(layer, x_ref, pos_ref, freq_ref, ids_ref, again_ref, qgain_ref, kgain_ref, mgain_ref, wr_ref, kc_hbm, vc_hbm, wq_hbm, wk_hbm, wv_hbm, wo_hbm, *rest):
    if layer:
        rest = rest[2:]
    (x_out, u_out, gate_out, ko_hbm, vo_hbm, wq, wk, wv, wo, kbuf, vbuf, q_rows, k_t, v_t, o_rows, cos_t, sin_t, score, w_sem, kin_sem, vin_sem, kout_sem, vout_sem) = rest
    heads, slots, dim, rows = kbuf.shape
    half = dim // 2
    w_copies = [pltpu.make_async_copy(src.at[layer], dst, w_sem.at[i]) for i, (src, dst) in enumerate(((wq_hbm, wq), (wk_hbm, wk), (wv_hbm, wv), (wo_hbm, wo)))]
    for copy in w_copies[:3]:
        copy.start()

    def cache_in(n):
        return (pltpu.make_async_copy(kc_hbm.at[layer, :, n], kbuf.at[n], kin_sem.at[n]), pltpu.make_async_copy(vc_hbm.at[layer, :, n], vbuf.at[n], vin_sem.at[n]))

    def cache_out(n):
        return (pltpu.make_async_copy(kbuf.at[n], ko_hbm.at[layer, :, n], kout_sem.at[n]), pltpu.make_async_copy(vbuf.at[n], vo_hbm.at[layer, :, n], vout_sem.at[n]))

    for n in range(heads):
        for copy in cache_in(n):
            copy.start()
    w_copies[3].start()

    pos = pos_ref[...]
    angles = pos.astype(F32) * freq_ref[...]
    cos_t[...] = jnp.cos(angles)
    sin_t[...] = jnp.sin(angles)
    normed = rms_scale(x_ref[...].astype(F32), again_ref[...]).astype(BF16)

    def rope(tensor):
        lo, hi = tensor[:half], tensor[half:]
        cos, sin = cos_t[...], sin_t[...]
        return jnp.concatenate([lo * cos - hi * sin, hi * cos + lo * sin], axis=0)

    w_copies[0].wait()
    q_rows[...] = rms_scale(jnp.dot(normed, wq[...], preferred_element_type=F32), qgain_ref[...])
    w_copies[1].wait()
    key_new = rms_scale(jnp.dot(normed, wk[...], preferred_element_type=F32), kgain_ref[...])
    w_copies[2].wait()
    value_new = jnp.dot(normed, wv[...], preferred_element_type=F32)
    pair = 2 * dim
    for c in range(heads // 2):
        chunk = key_new[:, c * pair:(c + 1) * pair].T
        for j in range(2):
            k_t[2 * c + j] = rope(chunk[j * dim:(j + 1) * dim]).astype(BF16)
        chunk = value_new[:, c * pair:(c + 1) * pair].T.astype(BF16)
        for j in range(2):
            v_t[2 * c + j] = chunk[j * dim:(j + 1) * dim]

    pos_b = jnp.broadcast_to(pos.astype(F32), (dim, rows)).astype(BF16)
    slot_ids = lax.broadcasted_iota(jnp.int32, (slots, rows), 0)

    def one_head(n, carry):
        cols = pl.ds(pl.multiple_of(n * pair, pair), pair)
        qt = q_rows[:, cols].T
        q0 = rope(qt[:dim]).astype(BF16).astype(F32) * dim ** -0.5
        q1 = rope(qt[dim:]).astype(BF16).astype(F32) * dim ** -0.5
        k_new, v_new = k_t[n], v_t[n]
        k_in, v_in = cache_in(n)
        k_in.wait()
        for s in range(slots):
            key = jnp.where(pos_b == s, k_new, kbuf[n, s])
            kbuf[n, s] = key
            key = key.astype(F32)
            score[0, s:s + 1] = jnp.sum(key * q0, axis=0, keepdims=True)
            score[1, s:s + 1] = jnp.sum(key * q1, axis=0, keepdims=True)
        k_out, v_out = cache_out(n)
        k_out.start()
        for g in range(2):
            masked = jnp.where(slot_ids <= pos, score[g], -jnp.inf)
            weight = jnp.exp(masked - jnp.max(masked, axis=0, keepdims=True))
            score[g] = (weight / jnp.sum(weight, axis=0, keepdims=True)).astype(BF16).astype(F32)
        v_in.wait()
        acc0 = jnp.zeros((dim, rows), F32)
        acc1 = jnp.zeros((dim, rows), F32)
        for s in range(slots):
            value = jnp.where(pos_b == s, v_new, vbuf[n, s])
            vbuf[n, s] = value
            value = value.astype(F32)
            acc0 += value * score[0, s:s + 1]
            acc1 += value * score[1, s:s + 1]
        v_out.start()
        o_rows[:, cols] = jnp.concatenate([acc0, acc1], axis=0).T.astype(BF16)
        return carry

    lax.fori_loop(0, heads, one_head, 0)
    w_copies[3].wait()
    x_new = (x_ref[...].astype(F32) + jnp.dot(o_rows[...], wo[...], preferred_element_type=F32)).astype(BF16)
    x_out[...] = x_new
    u = rms_scale(x_new.astype(F32), mgain_ref[...]).astype(BF16)
    u_out[...] = u
    logits = lax.dot_general(wr_ref[...], u, (((1,), (1,)), ((), ())), preferred_element_type=F32)
    weight = jnp.exp(logits - jnp.max(logits, axis=0, keepdims=True))
    probs = weight / jnp.sum(weight, axis=0, keepdims=True)
    expert_ids = lax.broadcasted_iota(jnp.int32, probs.shape, 0)
    member = expert_ids == ids_ref[0:1]
    for j in range(1, ids_ref.shape[0]):
        member = member | (expert_ids == ids_ref[j:j + 1])
    gate_out[...] = jnp.where(member, probs, 0.0)
    for n in range(heads):
        for copy in cache_out(n):
            copy.wait()


def attention_call(layer, x, pos, freq, ids, again, qgain, kgain, mgain, wr, kc, vc, wq, wk, wv, wo, prev):
    layers, slots, heads, dim, rows = kc.shape
    hidden = x.shape[1]
    experts = wr.shape[0]
    q_width, kv_width = wq.shape[2], wk.shape[2]
    vmem, hbm = pl.BlockSpec(memory_space=pltpu.VMEM), pl.BlockSpec(memory_space=pl.ANY)
    args = (x, pos, freq, ids, again, qgain, kgain, mgain, wr, kc, vc, wq, wk, wv, wo) + tuple(prev)
    return pl.pallas_call(
        functools.partial(attention_kernel, layer),
        name=f"attention_{layer}",
        out_shape=(
            jax.ShapeDtypeStruct((rows, hidden), BF16),
            jax.ShapeDtypeStruct((rows, hidden), BF16),
            jax.ShapeDtypeStruct((experts, rows), F32),
            jax.ShapeDtypeStruct(kc.shape, kc.dtype),
            jax.ShapeDtypeStruct(vc.shape, vc.dtype),
        ),
        in_specs=[vmem] * 9 + [hbm] * (len(args) - 9),
        out_specs=(vmem, vmem, vmem, hbm, hbm),
        scratch_shapes=[
            pltpu.VMEM((hidden, q_width), BF16),
            pltpu.VMEM((hidden, kv_width), BF16),
            pltpu.VMEM((hidden, kv_width), BF16),
            pltpu.VMEM((q_width, hidden), BF16),
            pltpu.VMEM((heads, slots, dim, rows), BF16),
            pltpu.VMEM((heads, slots, dim, rows), BF16),
            pltpu.VMEM((rows, q_width), F32),
            pltpu.VMEM((heads, dim, rows), BF16),
            pltpu.VMEM((heads, dim, rows), BF16),
            pltpu.VMEM((rows, q_width), BF16),
            pltpu.VMEM((dim // 2, rows), F32),
            pltpu.VMEM((dim // 2, rows), F32),
            pltpu.VMEM((2, slots, rows), F32),
            pltpu.SemaphoreType.DMA((4,)),
            pltpu.SemaphoreType.DMA((heads,)),
            pltpu.SemaphoreType.DMA((heads,)),
            pltpu.SemaphoreType.DMA((heads,)),
            pltpu.SemaphoreType.DMA((heads,)),
        ],
        input_output_aliases={15: 3, 16: 4} if prev else {},
        compiler_params=pltpu.CompilerParams(vmem_limit_bytes=VMEM_LIMIT),
    )(*args)


def moe_kernel(layer, u_ref, gate_ref, x_ref, wg_hbm, wu_hbm, wd_hbm, out_ref, wg, wu, wd, ag_u, ag_g, part, psib, rs_in, w_sem, agu_send, agu_recv, sbu_send, sbu_recv, agg_send, agg_recv, sbg_send, sbg_recv, ps_send, ps_recv, rs_send, rs_recv):
    steps, _, rows, hidden = part.shape
    me = lax.axis_index("ep")
    core, chip = me % 2, me // 2
    chip_z, chip_y = chip // 2, chip % 2
    place = chip_y * (steps - 1 - chip_z) + (1 - chip_y) * chip_z

    def device_at(p, c):
        far = p // (steps // 2)
        z = (1 - far) * p + far * (steps - 1 - p)
        return (z * 2 + far) * 2 + c

    nxt = device_at((place + 1 - 2 * core + steps) % steps, core)
    prv = device_at((place - 1 + 2 * core + steps) % steps, core)
    sib = chip * 2 + (1 - core)

    w_copies = [pltpu.make_async_copy(src.at[layer], dst, w_sem.at[i]) for i, (src, dst) in enumerate(((wg_hbm, wg), (wu_hbm, wu), (wd_hbm, wd)))]
    for copy in w_copies:
        copy.start()
    barrier = pltpu.get_barrier_semaphore()
    for peer in (prv, sib):
        pl.semaphore_signal(barrier, inc=1, device_id={"ep": peer}, device_id_type=MESH)

    def remote(src, dst, send, recv, peer):
        return pltpu.make_async_remote_copy(src_ref=src, dst_ref=dst, send_sem=send, recv_sem=recv, device_id={"ep": peer}, device_id_type=MESH)

    ag_rows = rows // AG_SUBS
    rs_rows = rows // RS_SUBS

    def ring_u(k, s, src=None):
        span = pl.ds(s * ag_rows, ag_rows)
        src = ag_u.at[k, 0, span] if src is None else src.at[span]
        return remote(src, ag_u.at[k + 1, 0, span], agu_send.at[k, s], agu_recv.at[k + 1, s], nxt)

    def sib_u(k, s, src=None):
        span = pl.ds(s * ag_rows, ag_rows)
        src = ag_u.at[k, 0, span] if src is None else src.at[span]
        return remote(src, ag_u.at[k, 1, span], sbu_send.at[k, s], sbu_recv.at[k, s], sib)

    def ring_g(k, src=None):
        return remote(ag_g.at[k, 0] if src is None else src, ag_g.at[k + 1, 0], agg_send.at[k], agg_recv.at[k + 1], nxt)

    def sib_g(k, src=None):
        return remote(ag_g.at[k, 0] if src is None else src, ag_g.at[k, 1], sbg_send.at[k], sbg_recv.at[k], sib)

    def sib_part(k, s):
        span = pl.ds(s * rs_rows, rs_rows)
        return remote(part.at[k, 1, span], psib.at[k, span], ps_send.at[k, s], ps_recv.at[k, s], sib)

    def ring_part(k, s):
        span = pl.ds(s * rs_rows, rs_rows)
        return remote(part.at[k, 0, span], rs_in.at[k, span], rs_send.at[k, s], rs_recv.at[k, s], nxt)

    pl.semaphore_wait(barrier, 2)
    ring_g(0, gate_ref).start()
    for s in range(AG_SUBS):
        ring_u(0, s, u_ref).start()
    sib_g(0, gate_ref).start()
    for s in range(AG_SUBS):
        sib_u(0, s, u_ref).start()
    ag_u[0, 0] = u_ref[...]
    ag_g[0, 0] = gate_ref[...]

    def take_block(k):
        ring_g(k - 1).wait_recv()

        @pl.when(k < steps - 1)
        def _():
            ring_g(k).start()

        sib_g(k).start()
        for s in range(AG_SUBS):
            ring_u(k - 1, s).wait_recv()

            @pl.when(k < steps - 1)
            def _():
                ring_u(k, s).start()

            sib_u(k, s).start()

    def add_sub(k, s, first):
        span = pl.ds(s * rs_rows, rs_rows)
        sib_part(k, s).wait_recv()
        total = part[k, 0, span] + psib[k, span]
        if not first:
            ring_part(k - 1, s).wait_recv()
            total += rs_in[k - 1, span]
        part[k, 0, span] = total
        ring_part(k, s).start()

    lane = lax.broadcasted_iota(jnp.int32, (rows, gate_ref.shape[0]), 1)
    for copy in w_copies:
        copy.wait()

    def one_step(k, carry):
        sib_g(k).wait_recv()
        for s in range(AG_SUBS):
            sib_u(k, s).wait_recv()
        block = ag_u[k].reshape(2 * rows, hidden)
        gates = [ag_g[k, j].T for j in range(2)]
        piece = 0

        def reduce_piece(s):
            @pl.when(k == 2)
            def _():
                add_sub(k - 1, s, True)

            @pl.when(k > 2)
            def _():
                add_sub(k - 1, s, False)

        for e in range(2):
            gate_part = jnp.dot(block, wg[e], preferred_element_type=F32)
            up_part = jnp.dot(block, wu[e], preferred_element_type=F32)
            weight = jnp.concatenate([jnp.sum(jnp.where(lane == 2 * me + e, g, 0.0), axis=1, keepdims=True) for g in gates], axis=0)
            activated = jnp.where(weight != 0.0, jax.nn.silu(gate_part) * up_part, 0.0).astype(BF16)
            reduce_piece(2 * e)
            if e == 1:
                @pl.when(k < steps - 1)
                def _():
                    take_block(k + 1)

            expert_out = jnp.dot(activated, wd[e], preferred_element_type=F32).astype(BF16).astype(F32) * weight
            expert_out = expert_out.reshape(2, rows, hidden)
            if e == 0:
                part[k] = expert_out
            else:
                part[k] += expert_out
            reduce_piece(2 * e + 1)
        for s in range(RS_SUBS):
            sib_part(k, s).start()
        return carry

    lax.fori_loop(0, steps, one_step, 0)
    for s in range(RS_SUBS):
        add_sub(steps - 1, s, False)
    for s in range(RS_SUBS):
        span = pl.ds(s * rs_rows, rs_rows)
        sib_part(0, s).wait_recv()
        own = part[0, 0, span] + psib[0, span]
        ring_part(steps - 1, s).wait_recv()
        out_ref[span] = (x_ref[span].astype(F32) + (own + rs_in[steps - 1, span])).astype(BF16)

    def drain(k, carry):
        sib_g(k).wait_send()
        for s in range(AG_SUBS):
            sib_u(k, s).wait_send()
        for s in range(RS_SUBS):
            sib_part(k, s).wait_send()

        @pl.when(k < steps - 1)
        def _():
            ring_g(k).wait_send()
            for s in range(AG_SUBS):
                ring_u(k, s).wait_send()
            for s in range(RS_SUBS):
                ring_part(k + 1, s).wait_send()

        return carry

    lax.fori_loop(0, steps, drain, 0)


def moe_call(layer, u, gate, x, wg, wu, wd, steps):
    rows, hidden = u.shape
    experts = gate.shape[0]
    width = wg.shape[3]
    vmem, hbm = pl.BlockSpec(memory_space=pltpu.VMEM), pl.BlockSpec(memory_space=pl.ANY)
    dma = pltpu.SemaphoreType.DMA
    return pl.pallas_call(
        functools.partial(moe_kernel, layer),
        name=f"moe_{layer}",
        out_shape=jax.ShapeDtypeStruct((rows, hidden), BF16),
        in_specs=[vmem] * 3 + [hbm] * 3,
        out_specs=vmem,
        scratch_shapes=[
            pltpu.VMEM((2, hidden, width), BF16),
            pltpu.VMEM((2, hidden, width), BF16),
            pltpu.VMEM((2, width, hidden), BF16),
            pltpu.VMEM((steps, 2, rows, hidden), BF16),
            pltpu.VMEM((steps, 2, experts, rows), F32),
            pltpu.VMEM((steps, 2, rows, hidden), F32),
            pltpu.VMEM((steps, rows, hidden), F32),
            pltpu.VMEM((steps, rows, hidden), F32),
            dma((3,)),
            dma((steps, AG_SUBS)), dma((steps, AG_SUBS)), dma((steps, AG_SUBS)), dma((steps, AG_SUBS)),
            dma((steps,)), dma((steps,)), dma((steps,)), dma((steps,)),
            dma((steps, RS_SUBS)), dma((steps, RS_SUBS)), dma((steps, RS_SUBS)), dma((steps, RS_SUBS)),
        ],
        compiler_params=pltpu.CompilerParams(vmem_limit_bytes=VMEM_LIMIT, collective_id=layer, has_side_effects=True),
    )(u, gate, x, wg, wu, wd)


def solution(mesh):
    group_size = mesh.shape['ep']
    seq_axes = ('dp', 'ep')

    def device_step(hidden_state, key_cache, value_cache, positions, expert_ids, attn_gain, w_query, w_key, w_value, q_gain, k_gain, w_out, moe_gain, w_router, w_gate, w_up, w_down):
        dim = key_cache.shape[-1]
        rows = hidden_state.shape[0]
        freq = ROPE_THETA ** (-jnp.arange(0, dim, 2, dtype=F32) / dim)
        freq = jnp.broadcast_to(freq[:, None], (dim // 2, rows))
        keys = jnp.transpose(key_cache, (0, 2, 3, 4, 1))
        values = jnp.transpose(value_cache, (0, 2, 3, 4, 1))
        ids = jnp.transpose(expert_ids, (0, 2, 1))
        router = jnp.transpose(w_router, (0, 2, 1))
        pos = positions[None, :]
        hidden_x = hidden_state
        prev = ()
        for layer in range(key_cache.shape[0]):
            row = slice(layer, layer + 1)
            hidden_x, u, gate, *prev = attention_call(layer, hidden_x, pos, freq, ids[layer], attn_gain[row], q_gain[row], k_gain[row], moe_gain[row], router[layer], keys, values, w_query, w_key, w_value, w_out, prev)
            hidden_x = moe_call(layer, u, gate, hidden_x, w_gate, w_up, w_down, group_size // 2)
        return hidden_x, jnp.transpose(prev[0], (0, 4, 1, 2, 3)), jnp.transpose(prev[1], (0, 4, 1, 2, 3))

    cache_spec = P(None, seq_axes, None, None, None)
    expert_spec = P(None, 'ep', None, None)
    in_specs = (P(seq_axes, None), cache_spec, cache_spec, P(seq_axes), P(None, seq_axes, None)) + (P(),) * 9 + (expert_spec,) * 3
    out_specs = (P(seq_axes, None), cache_spec, cache_spec)
    return jax.shard_map(device_step, mesh=mesh, in_specs=in_specs, out_specs=out_specs, check_vma=False)
```

time: 1040 us -> 180 us (0.17)
  the two profiles are of different devices: /device:TPU:15 before, /device:TPU:0 now
where the time goes in v1:
time: 180 us
  Pallas kernels  170 us (94%)
  local copies, waits for them, and re-layouts  9.3 us (5%)
    pallas_call x2, Pallas kernels, moe_call(): pl.pallas_call(functools.partial(moe_kernel, layer), name=f'moe_{layer}',...  143 us
    pallas_call x2, Pallas kernels, attention_call(): pl.pallas_call(functools.partial(attention_kernel, layer), name=f'attenti...  26.8 us

profile of v1, /device:TPU:0, one launch (start us, length us, event | category | flops | bytes accessed | tf_op | source)
XLA Modules:
  0.0 179.9 jit_solution(5412226936354650668)
XLA Ops:
  0.6 1.4 fusion.3
  2.0 1.3 slice_bitcast_fusion.2
  3.3 1.4 fusion.2
  4.7 0.7 broadcast_in_dim.12.freq_ref
  5.3 1.4 fusion
  6.7 1.5 slice_bitcast_fusion
  8.3 13.4 %attention_0.1 = (bf16[128,1024]{1,0:T(8,128)(2,1)}, bf16[128,1024]{1,0:T(8,128)(2,1)}, f32[32,128]{1,0:T(8,128)}, bf16[2,32,8,64,128]{4,3,2,1,0:T(8,128)(2,1)}, bf16[2,32,8,64,128]{4,3,2,1,0:T(8,128)(2,1)}) custom-call(bf16[128,1024]{1,0:T(8,128)(2,1)} %x_ref.1, s32[1,128]{1,0:T(1,128)} %bitcast.23, f32[32,128]{1,0:T(8,128)} %broadcast_in_dim.12.freq_ref, ...), custom_call_target="tpu_custom_call" | custom-call | tf_op jit(solution)/shard_map/attention_0/pallas_call | solution.py:134
  21.7 72.3 %moe_0.1.x_ref = bf16[128,1024]{1,0:T(8,128)(2,1)} custom-call(bf16[128,1024]{1,0:T(8,128)(2,1)} %get-tuple-element.13.u_ref, f32[32,128]{1,0:T(8,128)} %get-tuple-element.14.gate_ref, bf16[128,1024]{1,0:T(8,128)(2,1)} %get-tuple-element.15.x_ref, bf16[2,2,1024,512]{3,2,1,0:T(8,128)(2,1)} %wg_hbm.3, bf16[2,2,1024,512]{3,2,1,0:T(8,128)(2,1)} %wu_hbm.3, ...), custom_call_target="tpu_custom_call" | custom-call | tf_op jit(solution)/shard_map/moe_0/pallas_call | solution.py:340
  94.0 13.4 %attention_1.1 = (bf16[128,1024]{1,0:T(8,128)(2,1)}, bf16[128,1024]{1,0:T(8,128)(2,1)}, f32[32,128]{1,0:T(8,128)}, bf16[2,32,8,64,128]{4,3,2,1,0:T(8,128)(2,1)}, bf16[2,32,8,64,128]{4,3,2,1,0:T(8,128)(2,1)}) custom-call(bf16[128,1024]{1,0:T(8,128)(2,1)} %moe_0.1.x_ref, s32[1,128]{1,0:T(1,128)} %bitcast.24, ...), custom_call_target="tpu_custom_call", output_to_operand_aliasing={{3}: (15, {}), {4}: (16, {})} | custom-call | tf_op jit(solution)/shard_map/attention_1/pallas_call | solution.py:134
  107.4 70.8 %moe_1.1 = bf16[128,1024]{1,0:T(8,128)(2,1)} custom-call(bf16[128,1024]{1,0:T(8,128)(2,1)} %get-tuple-element.18.u_ref, f32[32,128]{1,0:T(8,128)} %get-tuple-element.19.gate_ref, bf16[128,1024]{1,0:T(8,128)(2,1)} %get-tuple-element.20.x_ref, bf16[2,2,1024,512]{3,2,1,0:T(8,128)(2,1)} %wg_hbm.3, bf16[2,2,1024,512]{3,2,1,0:T(8,128)(2,1)} %wu_hbm.3, ...), custom_call_target="tpu_custom_call" | custom-call | tf_op jit(solution)/shard_map/moe_1/pallas_call | solution.py:340
  178.2 1.7 copy.25
  (1 shorter events, 0.0 us)

commit v2 on v1

v2 whole, which is shorter than its diff:
```python
import functools

import jax
import jax.numpy as jnp
from jax import lax
from jax.experimental import pallas as pl
from jax.experimental.pallas import tpu as pltpu
from jax.sharding import PartitionSpec as P
import numpy as np

NORM_EPS = 1e-5
ROPE_THETA = 10000.0
F32 = jnp.float32
BF16 = jnp.bfloat16
MESH = pl.DeviceIdType.MESH
RS_SUBS = 4
AG_SUBS = 4
ATTENTION_VMEM = 16 * 1024 * 1024
MOE_VMEM = 32 * 1024 * 1024


def rms_scale(tensor, gain):
    mean_sq = jnp.mean(tensor * tensor, axis=-1, keepdims=True)
    return tensor * lax.rsqrt(mean_sq + NORM_EPS) * gain


def attention_kernel(layer, *rest):
    small, rest = rest[:9], rest[9:]
    if layer:
        (k_raw, v_raw, wq, wk, wv, wo, k_first, v_first, x_out, u_out, gate_out, ko_hbm, vo_hbm, kbuf, vbuf, q_rows, k_t, v_t, o_rows, cos_t, sin_t, score, first_sem, cache_sem) = rest
    else:
        (kc_hbm, vc_hbm, wq_hbm, wk_hbm, wv_hbm, wo_hbm, x_out, u_out, gate_out, kbuf, vbuf, wq, wk, wv, wo, q_rows, k_t, v_t, o_rows, cos_t, sin_t, score, w_sem, cache_sem, *held, small_sem) = rest
        k_raw, v_raw = kbuf, vbuf
        small_copies = [pltpu.make_async_copy(src, dst, small_sem.at[i]) for i, (src, dst) in enumerate(zip(small, held))]
        small = held
        for copy in small_copies:
            copy.start()
    x_ref, again_ref, pos_ref, freq_ref, qgain_ref, kgain_ref, mgain_ref, ids_ref, wr_ref = small
    heads, slots, dim, rows = kbuf.shape
    half = dim // 2
    row = slice(layer, layer + 1)
    if layer:
        first_out = [pltpu.make_async_copy(src.at[n], dst.at[0, :, n], first_sem.at[i, n]) for n in range(heads) for i, (src, dst) in enumerate(((k_first, ko_hbm), (v_first, vo_hbm)))]
        for copy in first_out:
            copy.start()
    else:
        w_copies = [pltpu.make_async_copy(src.at[layer], dst, w_sem.at[i]) for i, (src, dst) in enumerate(((wq_hbm, wq), (wk_hbm, wk), (wv_hbm, wv), (wo_hbm, wo)))]
        for copy in w_copies[:3]:
            copy.start()

    def cache_copies(n):
        if layer:
            return (pltpu.make_async_copy(kbuf.at[n], ko_hbm.at[layer, :, n], cache_sem.at[0, n]), pltpu.make_async_copy(vbuf.at[n], vo_hbm.at[layer, :, n], cache_sem.at[1, n]))
        return (pltpu.make_async_copy(kc_hbm.at[layer, :, n], kbuf.at[n], cache_sem.at[0, n]), pltpu.make_async_copy(vc_hbm.at[layer, :, n], vbuf.at[n], cache_sem.at[1, n]))

    if not layer:
        for n in range(heads):
            for copy in cache_copies(n):
                copy.start()
        w_copies[3].start()

    if not layer:
        for copy in small_copies[:4]:
            copy.wait()
    pos = pos_ref[...]
    angles = pos.astype(F32) * freq_ref[...]
    cos_t[...] = jnp.cos(angles)
    sin_t[...] = jnp.sin(angles)
    normed = rms_scale(x_ref[...].astype(F32), again_ref[row]).astype(BF16)

    def rope(tensor):
        lo, hi = tensor[:half], tensor[half:]
        cos, sin = cos_t[...], sin_t[...]
        return jnp.concatenate([lo * cos - hi * sin, hi * cos + lo * sin], axis=0)

    if not layer:
        for copy in small_copies[4:]:
            copy.wait()
        w_copies[0].wait()
    q_rows[...] = rms_scale(jnp.dot(normed, wq[...], preferred_element_type=F32), qgain_ref[row])
    if not layer:
        w_copies[1].wait()
    key_new = rms_scale(jnp.dot(normed, wk[...], preferred_element_type=F32), kgain_ref[row])
    if not layer:
        w_copies[2].wait()
    value_new = jnp.dot(normed, wv[...], preferred_element_type=F32)
    pair = 2 * dim
    for c in range(heads // 2):
        chunk = key_new[:, c * pair:(c + 1) * pair].T
        for j in range(2):
            k_t[2 * c + j] = rope(chunk[j * dim:(j + 1) * dim]).astype(BF16)
        chunk = value_new[:, c * pair:(c + 1) * pair].T.astype(BF16)
        for j in range(2):
            v_t[2 * c + j] = chunk[j * dim:(j + 1) * dim]

    pos_b = jnp.broadcast_to(pos.astype(F32), (dim, rows)).astype(BF16)
    slot_ids = lax.broadcasted_iota(jnp.int32, (slots, rows), 0)

    def one_head(n, carry):
        cols = pl.ds(pl.multiple_of(n * pair, pair), pair)
        qt = q_rows[:, cols].T
        q0 = rope(qt[:dim]).astype(BF16).astype(F32) * dim ** -0.5
        q1 = rope(qt[dim:]).astype(BF16).astype(F32) * dim ** -0.5
        k_new, v_new = k_t[n], v_t[n]
        k_copy, v_copy = cache_copies(n)
        if not layer:
            k_copy.wait()
        for s in range(slots):
            key = jnp.where(pos_b == s, k_new, k_raw[n, s])
            kbuf[n, s] = key
            key = key.astype(F32)
            score[0, s:s + 1] = jnp.sum(key * q0, axis=0, keepdims=True)
            score[1, s:s + 1] = jnp.sum(key * q1, axis=0, keepdims=True)
        if layer:
            k_copy.start()
        for g in range(2):
            masked = jnp.where(slot_ids <= pos, score[g], -jnp.inf)
            weight = jnp.exp(masked - jnp.max(masked, axis=0, keepdims=True))
            score[g] = (weight / jnp.sum(weight, axis=0, keepdims=True)).astype(BF16).astype(F32)
        if not layer:
            v_copy.wait()
        acc0 = jnp.zeros((dim, rows), F32)
        acc1 = jnp.zeros((dim, rows), F32)
        for s in range(slots):
            value = jnp.where(pos_b == s, v_new, v_raw[n, s])
            vbuf[n, s] = value
            value = value.astype(F32)
            acc0 += value * score[0, s:s + 1]
            acc1 += value * score[1, s:s + 1]
        if layer:
            v_copy.start()
        o_rows[:, cols] = jnp.concatenate([acc0, acc1], axis=0).T.astype(BF16)
        return carry

    lax.fori_loop(0, heads, one_head, 0)
    if not layer:
        w_copies[3].wait()
    x_new = (x_ref[...].astype(F32) + jnp.dot(o_rows[...], wo[...], preferred_element_type=F32)).astype(BF16)
    x_out[...] = x_new
    u = rms_scale(x_new.astype(F32), mgain_ref[row]).astype(BF16)
    u_out[...] = u
    logits = lax.dot_general(wr_ref[layer], u, (((1,), (1,)), ((), ())), preferred_element_type=F32)
    weight = jnp.exp(logits - jnp.max(logits, axis=0, keepdims=True))
    probs = weight / jnp.sum(weight, axis=0, keepdims=True)
    expert_ids = lax.broadcasted_iota(jnp.int32, probs.shape, 0)
    member = expert_ids == ids_ref[layer, 0:1]
    for j in range(1, ids_ref.shape[1]):
        member = member | (expert_ids == ids_ref[layer, j:j + 1])
    gate_out[...] = jnp.where(member, probs, 0.0)
    if layer:
        for copy in first_out:
            copy.wait()
        for n in range(heads):
            for copy in cache_copies(n):
                copy.wait()


def attention_call(layer, x, pos, freq, ids, again, qgain, kgain, mgain, wr, kc, vc, wq, wk, wv, wo, ready):
    layers, slots, heads, dim, rows = kc.shape
    hidden = x.shape[1]
    experts = wr.shape[1]
    q_width, kv_width = wq.shape[2], wk.shape[2]
    vmem, hbm = pl.BlockSpec(memory_space=pltpu.VMEM), pl.BlockSpec(memory_space=pltpu.HBM)
    small = (x, again, pos, freq, qgain, kgain, mgain, ids, wr)
    out_shape = [
        jax.ShapeDtypeStruct((rows, hidden), BF16),
        jax.ShapeDtypeStruct((rows, hidden), BF16),
        jax.ShapeDtypeStruct((experts, rows), F32),
    ]
    cache = pltpu.VMEM((heads, slots, dim, rows), BF16)
    dma = pltpu.SemaphoreType.DMA
    scratch = [
        pltpu.VMEM((rows, q_width), F32),
        pltpu.VMEM((heads, dim, rows), BF16),
        pltpu.VMEM((heads, dim, rows), BF16),
        pltpu.VMEM((rows, q_width), BF16),
        pltpu.VMEM((dim // 2, rows), F32),
        pltpu.VMEM((dim // 2, rows), F32),
        pltpu.VMEM((2, slots, rows), F32),
    ]
    if layer:
        args = small + tuple(pltpu.with_memory_space_constraint(a, pltpu.VMEM) for a in ready)
        in_specs = [vmem] * len(args)
        out_shape += [jax.ShapeDtypeStruct(kc.shape, kc.dtype), jax.ShapeDtypeStruct(vc.shape, vc.dtype)]
        out_specs = [vmem] * 3 + [hbm] * 2
        scratch = [cache, cache] + scratch + [dma((2, heads)), dma((2, heads))]
    else:
        args = tuple(pltpu.with_memory_space_constraint(a, pltpu.HBM) for a in small) + (kc, vc, wq, wk, wv, wo)
        in_specs = [hbm] * len(args)
        out_shape += [cache, cache]
        out_specs = [vmem] * 5
        scratch = [pltpu.VMEM(w.shape[1:], BF16) for w in (wq, wk, wv, wo)] + scratch + [dma((4,)), dma((2, heads))] + [pltpu.VMEM(a.shape, a.dtype) for a in small] + [dma((len(small),))]
    return pl.pallas_call(
        functools.partial(attention_kernel, layer),
        name=f"attention_{layer}",
        out_shape=out_shape,
        in_specs=in_specs,
        out_specs=out_specs,
        scratch_shapes=scratch,
        compiler_params=pltpu.CompilerParams(vmem_limit_bytes=ATTENTION_VMEM),
    )(*args)


def moe_kernel(layer, n_ahead, u_ref, gate_ref, x_ref, wg_hbm, wu_hbm, wd_hbm, *rest):
    ahead_hbm, out_ref, ahead, rest = rest[:n_ahead], rest[n_ahead], rest[n_ahead + 1:2 * n_ahead + 1], rest[2 * n_ahead + 1:]
    (wg, wu, wd, ag_u, ag_g, part, psib, rs_in, w_sem, agu_send, agu_recv, sbu_send, sbu_recv, agg_send, agg_recv, sbg_send, sbg_recv, ps_send, ps_recv, rs_send, rs_recv, ahead_sem) = rest
    steps, _, rows, hidden = part.shape
    me = lax.axis_index("ep")
    core, chip = me % 2, me // 2
    chip_z, chip_y = chip // 2, chip % 2
    place = chip_y * (steps - 1 - chip_z) + (1 - chip_y) * chip_z

    def device_at(p, c):
        far = p // (steps // 2)
        z = (1 - far) * p + far * (steps - 1 - p)
        return (z * 2 + far) * 2 + c

    nxt = device_at((place + 1 - 2 * core + steps) % steps, core)
    prv = device_at((place - 1 + 2 * core + steps) % steps, core)
    sib = chip * 2 + (1 - core)

    w_copies = [pltpu.make_async_copy(src.at[layer], dst, w_sem.at[i]) for i, (src, dst) in enumerate(((wg_hbm, wg), (wu_hbm, wu), (wd_hbm, wd)))]
    for copy in w_copies:
        copy.start()
    barrier = pltpu.get_barrier_semaphore()
    for peer in (prv, sib):
        pl.semaphore_signal(barrier, inc=1, device_id={"ep": peer}, device_id_type=MESH)

    def remote(src, dst, send, recv, peer):
        return pltpu.make_async_remote_copy(src_ref=src, dst_ref=dst, send_sem=send, recv_sem=recv, device_id={"ep": peer}, device_id_type=MESH)

    ag_rows = rows // AG_SUBS
    rs_rows = rows // RS_SUBS

    def ring_u(k, s, src=None):
        span = pl.ds(s * ag_rows, ag_rows)
        src = ag_u.at[k, 0, span] if src is None else src.at[span]
        return remote(src, ag_u.at[k + 1, 0, span], agu_send.at[k, s], agu_recv.at[k + 1, s], nxt)

    def sib_u(k, s, src=None):
        span = pl.ds(s * ag_rows, ag_rows)
        src = ag_u.at[k, 0, span] if src is None else src.at[span]
        return remote(src, ag_u.at[k, 1, span], sbu_send.at[k, s], sbu_recv.at[k, s], sib)

    def ring_g(k, src=None):
        return remote(ag_g.at[k, 0] if src is None else src, ag_g.at[k + 1, 0], agg_send.at[k], agg_recv.at[k + 1], nxt)

    def sib_g(k, src=None):
        return remote(ag_g.at[k, 0] if src is None else src, ag_g.at[k, 1], sbg_send.at[k], sbg_recv.at[k], sib)

    def sib_part(k, s):
        span = pl.ds(s * rs_rows, rs_rows)
        return remote(part.at[k, 1, span], psib.at[k, span], ps_send.at[k, s], ps_recv.at[k, s], sib)

    def ring_part(k, s):
        span = pl.ds(s * rs_rows, rs_rows)
        return remote(part.at[k, 0, span], rs_in.at[k, span], rs_send.at[k, s], rs_recv.at[k, s], nxt)

    pl.semaphore_wait(barrier, 2)
    ring_g(0, gate_ref).start()
    for s in range(AG_SUBS):
        ring_u(0, s, u_ref).start()
    sib_g(0, gate_ref).start()
    for s in range(AG_SUBS):
        sib_u(0, s, u_ref).start()
    ag_u[0, 0] = u_ref[...]
    ag_g[0, 0] = gate_ref[...]

    def take_sub(k, s):
        if s == 0:
            ring_g(k - 1).wait_recv()

            @pl.when(k < steps - 1)
            def _():
                ring_g(k).start()

            sib_g(k).start()
        ring_u(k - 1, s).wait_recv()

        @pl.when(k < steps - 1)
        def _():
            ring_u(k, s).start()

        sib_u(k, s).start()

    def add_sub(k, s, first):
        span = pl.ds(s * rs_rows, rs_rows)
        sib_part(k, s).wait_recv()
        total = part[k, 0, span] + psib[k, span]
        if not first:
            ring_part(k - 1, s).wait_recv()
            total += rs_in[k - 1, span]
        part[k, 0, span] = total
        ring_part(k, s).start()

    lane = lax.broadcasted_iota(jnp.int32, (rows, gate_ref.shape[0]), 1)
    for copy in w_copies:
        copy.wait()
    ahead_copies = []
    for i, (src, dst) in enumerate(zip(ahead_hbm, ahead)):
        if len(src.shape) == 3:
            ahead_copies.append(pltpu.make_async_copy(src.at[layer + 1], dst, ahead_sem.at[i, 0]))
        else:
            ahead_copies += [pltpu.make_async_copy(src.at[layer + 1, :, n], dst.at[n], ahead_sem.at[i, n]) for n in range(dst.shape[0])]
    for copy in ahead_copies:
        copy.start()

    def one_step(k, carry):
        def forward(s):
            @pl.when(k < steps - 1)
            def _():
                take_sub(k + 1, s)

        def reduce(s):
            @pl.when(k == 2)
            def _():
                add_sub(k - 1, s, True)

            @pl.when(k > 2)
            def _():
                add_sub(k - 1, s, False)

        forward(0)
        sib_g(k).wait_recv()
        for s in range(AG_SUBS):
            sib_u(k, s).wait_recv()
        block = ag_u[k].reshape(2 * rows, hidden)
        gates = [ag_g[k, j].T for j in range(2)]

        for e in range(2):
            gate_part = jnp.dot(block, wg[e], preferred_element_type=F32)
            up_part = jnp.dot(block, wu[e], preferred_element_type=F32)
            weight = jnp.concatenate([jnp.sum(jnp.where(lane == 2 * me + e, g, 0.0), axis=1, keepdims=True) for g in gates], axis=0)
            activated = jnp.where(weight != 0.0, jax.nn.silu(gate_part) * up_part, 0.0).astype(BF16)
            forward(2 * e + 1)
            reduce(2 * e)
            expert_out = jnp.dot(activated, wd[e], preferred_element_type=F32).astype(BF16).astype(F32) * weight
            expert_out = expert_out.reshape(2, rows, hidden)
            if e == 0:
                part[k] = expert_out
            else:
                part[k] += expert_out
            if e == 0:
                forward(2)
            reduce(2 * e + 1)
        for s in range(RS_SUBS):
            sib_part(k, s).start()
        return carry

    lax.fori_loop(0, steps, one_step, 0)
    for s in range(RS_SUBS):
        add_sub(steps - 1, s, False)
    for s in range(RS_SUBS):
        span = pl.ds(s * rs_rows, rs_rows)
        sib_part(0, s).wait_recv()
        own = part[0, 0, span] + psib[0, span]
        ring_part(steps - 1, s).wait_recv()
        out_ref[span] = (x_ref[span].astype(F32) + (own + rs_in[steps - 1, span])).astype(BF16)

    def drain(k, carry):
        sib_g(k).wait_send()
        for s in range(AG_SUBS):
            sib_u(k, s).wait_send()
        for s in range(RS_SUBS):
            sib_part(k, s).wait_send()

        @pl.when(k < steps - 1)
        def _():
            ring_g(k).wait_send()
            for s in range(AG_SUBS):
                ring_u(k, s).wait_send()
            for s in range(RS_SUBS):
                ring_part(k + 1, s).wait_send()

        return carry

    lax.fori_loop(0, steps, drain, 0)
    for copy in ahead_copies:
        copy.wait()


def moe_call(layer, u, gate, x, wg, wu, wd, steps, ahead):
    rows, hidden = u.shape
    experts = gate.shape[0]
    width = wg.shape[3]
    vmem, hbm = pl.BlockSpec(memory_space=pltpu.VMEM), pl.BlockSpec(memory_space=pltpu.HBM)
    dma = pltpu.SemaphoreType.DMA
    kept = [a.shape[1:] if a.ndim == 3 else (a.shape[2], a.shape[1]) + a.shape[3:] for a in ahead]
    return pl.pallas_call(
        functools.partial(moe_kernel, layer, len(ahead)),
        name=f"moe_{layer}",
        out_shape=[jax.ShapeDtypeStruct((rows, hidden), BF16)] + [pltpu.VMEM(shape, BF16) for shape in kept],
        in_specs=[vmem] * 3 + [hbm] * (3 + len(ahead)),
        out_specs=[vmem] * (1 + len(ahead)),
        scratch_shapes=[
            pltpu.VMEM((2, hidden, width), BF16),
            pltpu.VMEM((2, hidden, width), BF16),
            pltpu.VMEM((2, width, hidden), BF16),
            pltpu.VMEM((steps, 2, rows, hidden), BF16),
            pltpu.VMEM((steps, 2, experts, rows), F32),
            pltpu.VMEM((steps, 2, rows, hidden), F32),
            pltpu.VMEM((steps, rows, hidden), F32),
            pltpu.VMEM((steps, rows, hidden), F32),
            dma((3,)),
            dma((steps, AG_SUBS)), dma((steps, AG_SUBS)), dma((steps, AG_SUBS)), dma((steps, AG_SUBS)),
            dma((steps,)), dma((steps,)), dma((steps,)), dma((steps,)),
            dma((steps, RS_SUBS)), dma((steps, RS_SUBS)), dma((steps, RS_SUBS)), dma((steps, RS_SUBS)),
            dma((6, 8)),
        ],
        compiler_params=pltpu.CompilerParams(vmem_limit_bytes=MOE_VMEM, collective_id=layer, has_side_effects=True),
    )(u, gate, x, wg, wu, wd, *ahead)


def solution(mesh):
    group_size = mesh.shape['ep']
    seq_axes = ('dp', 'ep')

    def device_step(hidden_state, key_cache, value_cache, positions, expert_ids, attn_gain, w_query, w_key, w_value, q_gain, k_gain, w_out, moe_gain, w_router, w_gate, w_up, w_down):
        dim = key_cache.shape[-1]
        rows = hidden_state.shape[0]
        freq = np.float32(ROPE_THETA) ** (-np.arange(0, dim, 2, dtype=np.float32) / np.float32(dim))
        freq = np.ascontiguousarray(np.broadcast_to(freq.astype(np.float32)[:, None], (dim // 2, rows)))
        keys = jnp.transpose(key_cache, (0, 2, 3, 4, 1))
        values = jnp.transpose(value_cache, (0, 2, 3, 4, 1))
        ids = jnp.transpose(expert_ids, (0, 2, 1))
        router = jnp.transpose(w_router, (0, 2, 1))
        pos = positions[None, :]
        small = (pos, freq, ids, attn_gain, q_gain, k_gain, moe_gain, router)
        big = tuple(pltpu.with_memory_space_constraint(a, pltpu.HBM) for a in (keys, values, w_query, w_key, w_value, w_out))
        experts = tuple(pltpu.with_memory_space_constraint(a, pltpu.HBM) for a in (w_gate, w_up, w_down)) + (group_size // 2,)
        hidden_x, u, gate, *first = attention_call(0, hidden_state, *small, *big, ())
        hidden_x, *ready = moe_call(0, u, gate, hidden_x, *experts, big)
        hidden_x, u, gate, *prev = attention_call(1, hidden_x, *small, *big, (*ready, *first))
        hidden_x, = moe_call(1, u, gate, hidden_x, *experts, ())
        return hidden_x, jnp.transpose(prev[0], (0, 4, 1, 2, 3)), jnp.transpose(prev[1], (0, 4, 1, 2, 3))

    cache_spec = P(None, seq_axes, None, None, None)
    expert_spec = P(None, 'ep', None, None)
    in_specs = (P(seq_axes, None), cache_spec, cache_spec, P(seq_axes), P(None, seq_axes, None)) + (P(),) * 9 + (expert_spec,) * 3
    out_specs = (P(seq_axes, None), cache_spec, cache_spec)
    return jax.shard_map(device_step, mesh=mesh, in_specs=in_specs, out_specs=out_specs, check_vma=False)
```

time: 180 us -> 163 us (0.906)
  Pallas kernels: 170 us -> 161 us
  local copies, waits for them, and re-layouts: 9.3 us -> 0.76 us
    pallas_call x2, Pallas kernels: 26.8 us -> 21.7 us  [attention_call(): pl.pallas_call(functools.partial(attention_kernel, layer), name=f'attenti...]
    slice x3 -> x0, local copies, waits for them, and re-layouts: 4.11 us -> none  [the longest x1 1.38 us: device_step(): moe_gain[row]]
    pallas_call x2, Pallas kernels: 143 us -> 139 us  [moe_call(): pl.pallas_call(functools.partial(moe_kernel, layer, len(ahead)), name=f'm...]
    squeeze x2 -> x0, local copies, waits for them, and re-layouts: 2.84 us -> none  [the longest x1 1.54 us: device_step(): router[layer]]
where the time goes in v2:
time: 163 us; the launch traced here: 162 us
  Pallas kernels  161 us (99%)
    pallas_call x2, Pallas kernels, moe_call(): pl.pallas_call(functools.partial(moe_kernel, layer, len(ahead)), name=f'm...  139 us
    pallas_call x2, Pallas kernels, attention_call(): pl.pallas_call(functools.partial(attention_kernel, layer), name=f'attenti...  21.7 us

profile of v2, /device:TPU:0, one launch (start us, length us, event | category | flops | bytes accessed | tf_op | source)
XLA Modules:
  0.0 162.4 jit_solution(116724756352222284)
XLA Ops:
  0.6 13.1 %attention_0.1 = (bf16[128,1024]{1,0:T(8,128)(2,1)S(1)}, bf16[128,1024]{1,0:T(8,128)(2,1)S(1)}, f32[32,128]{1,0:T(8,128)S(1)}, bf16[8,32,64,128]{3,2,1,0:T(8,128)(2,1)S(1)}, bf16[8,32,64,128]{3,2,1,0:T(8,128)(2,1)S(1)}) custom-call(bf16[128,1024]{1,0:T(8,128)(2,1)} %rest_0_.1, f32[2,1024]{1,0:T(2,128)} %rest_1_.3, s32[1,128]{1,0:T(1,128)} %bitcast.11, ...), custom_call_target="tpu_custom_call" | custom-call | tf_op jit(solution)/shard_map/attention_0/pallas_call | solution.py:193
  13.8 0.0 copy-start
  13.8 0.0 copy-start.1
  13.8 0.0 copy-start.2
  13.8 0.0 copy-start.3
  13.8 0.0 copy-start.4
  13.8 0.0 copy-start.5
  13.8 0.0 copy-start.6
  13.9 0.0 copy-start.7
  13.9 71.1 %moe_0.1 = (bf16[128,1024]{1,0:T(8,128)(2,1)S(1)}, bf16[8,32,64,128]{3,2,1,0:T(8,128)(2,1)S(1)}, bf16[8,32,64,128]{3,2,1,0:T(8,128)(2,1)S(1)}, bf16[1024,1024]{1...) custom-call(bf16[128,1024]{1,0:T(8,128)(2,1)S(1)} %get-tuple-element, ...), custom_call_target="tpu_custom_call" | custom-call | tf_op jit(solution)/shard_map/moe_0/pallas_call | solution.py:389
  85.0 0.0 copy-done
  85.0 0.0 copy-done.1
  85.0 0.0 copy-done.2
  85.0 0.0 copy-done.3
  85.1 0.0 copy-done.4
  85.1 0.0 copy-done.5
  85.1 0.0 copy-done.6
  85.1 0.0 copy-done.7
  85.1 8.6 %attention_1.1 = (bf16[128,1024]{1,0:T(8,128)(2,1)S(1)}, bf16[128,1024]{1,0:T(8,128)(2,1)S(1)}, f32[32,128]{1,0:T(8,128)S(1)}, bf16[2,32,8,64,128]{4,3,2,1,0:T(8,128)(2,1)}, bf16[2,32,8,64,128]{4,3,2,1,0:T(8,128)(2,1)}) custom-call(bf16[128,1024]{1,0:T(8,128)(2,1)S(1)} %get-tuple-element.23.rest_0_, f32[2,1024]{1,0:T(2,128)S(1)} %copy-done.2, ...), custom_call_target="tpu_custom_call" | custom-call | tf_op jit(solution)/shard_map/attention_1/pallas_call | solution.py:193
  93.7 68.0 %moe_1.1 = bf16[128,1024]{1,0:T(8,128)(2,1)S(1)} custom-call(bf16[128,1024]{1,0:T(8,128)(2,1)S(1)} %get-tuple-element.32.u_ref, f32[32,128]{1,0:T(8,128)S(1)} %get-tuple-element.33.gate_ref, bf16[128,1024]{1,0:T(8,128)(2,1)S(1)} %get-tuple-element.34.x_ref, bf16[2,2,1024,512]{3,2,1,0:T(8,128)(2,1)} %wg_hbm.3, bf16[2,2,1024,512]{3,2,1,0:T(8,128)(2,1)} %wu_hbm.3, ...), custom_call_target="tpu_custom_call" | custom-call | tf_op jit(solution)/shard_map/moe_1/pallas_call | solution.py:389
  161.7 0.7 copy.22
Async XLA Ops:
  13.8 71.2 %copy-start = (bf16[2,1024,32]{1,2,0:T(8,128)(2,1)S(1)}, bf16[2,1024,32]{1,2,0:T(8,128)(2,1)}, u32[]{:S(2)}) copy-start(bf16[2,1024,32]{1,2,0:T(8,128)(2,1)} %param.31) | copy-start | bytes 393220
  13.8 71.2 %copy-start.1 = (f32[32,128]{1,0:T(8,128)S(1)}, f32[32,128]{1,0:T(8,128)}, u32[]{:S(2)}) copy-start(f32[32,128]{1,0:T(8,128)} %constant.2.clone.rest_3_) | copy-start | bytes 49156
  13.8 71.2 %copy-start.2 = (f32[2,1024]{1,0:T(2,128)S(1)}, f32[2,1024]{1,0:T(2,128)}, u32[]{:S(2)}) copy-start(f32[2,1024]{1,0:T(2,128)} %rest_1_.3) | copy-start | bytes 24580
  13.8 71.2 %copy-start.3 = (f32[2,1024]{1,0:T(2,128)S(1)}, f32[2,1024]{1,0:T(2,128)}, u32[]{:S(2)}) copy-start(f32[2,1024]{1,0:T(2,128)} %rest_4_.5) | copy-start | bytes 24580
  13.8 71.2 %copy-start.4 = (f32[2,1024]{1,0:T(2,128)S(1)}, f32[2,1024]{1,0:T(2,128)}, u32[]{:S(2)}) copy-start(f32[2,1024]{1,0:T(2,128)} %rest_6_.3) | copy-start | bytes 24580
  13.8 71.2 %copy-start.5 = (s32[2,128,8]{1,2,0:T(8,128)S(1)}, s32[2,128,8]{1,2,0:T(8,128)}, u32[]{:S(2)}) copy-start(s32[2,128,8]{1,2,0:T(8,128)} %param.22) | copy-start | bytes 24580
  13.8 71.2 %copy-start.6 = (f32[2,512]{1,0:T(2,128)S(1)}, f32[2,512]{1,0:T(2,128)}, u32[]{:S(2)}) copy-start(f32[2,512]{1,0:T(2,128)} %rest_5_.5) | copy-start | bytes 12292
  13.9 71.2 %copy-start.7 = (s32[128]{0:T(128)S(1)}, s32[128]{0:T(128)}, u32[]{:S(2)}) copy-start(s32[128]{0:T(128)} %param.21) | copy-start | bytes 1540

commit v3 on v2

--- a/solution.py
+++ b/solution.py
@@ -17,6 +17,11 @@
 AG_SUBS = 4
 ATTENTION_VMEM = 16 * 1024 * 1024
 MOE_VMEM = 32 * 1024 * 1024
+FIRST_VMEM = 31 * 1024 * 1024
+
+
+def turns(subs, part):
+    return range(part * subs // 4, (part + 1) * subs // 4)
 
 
 def rms_scale(tensor, gain):
@@ -24,7 +29,7 @@
     return tensor * lax.rsqrt(mean_sq + NORM_EPS) * gain
 
 
-def attention_kernel(layer, *rest):
+def attention_kernel(layer, *rest, loading=None):
     small, rest = rest[:9], rest[9:]
     if layer:
         (k_raw, v_raw, wq, wk, wv, wo, k_first, v_first, x_out, u_out, gate_out, ko_hbm, vo_hbm, kbuf, vbuf, q_rows, k_t, v_t, o_rows, cos_t, sin_t, score, first_sem, cache_sem) = rest
@@ -54,12 +59,6 @@
         return (pltpu.make_async_copy(kc_hbm.at[layer, :, n], kbuf.at[n], cache_sem.at[0, n]), pltpu.make_async_copy(vc_hbm.at[layer, :, n], vbuf.at[n], cache_sem.at[1, n]))
 
     if not layer:
-        for n in range(heads):
-            for copy in cache_copies(n):
-                copy.start()
-        w_copies[3].start()
-
-    if not layer:
         for copy in small_copies[:4]:
             copy.wait()
     pos = pos_ref[...]
@@ -77,12 +76,15 @@
         for copy in small_copies[4:]:
             copy.wait()
         w_copies[0].wait()
+        w_copies[1].wait()
+        w_copies[2].wait()
+        for n in range(heads):
+            for copy in cache_copies(n):
+                copy.start()
+        w_copies[3].start()
+        loading()
     q_rows[...] = rms_scale(jnp.dot(normed, wq[...], preferred_element_type=F32), qgain_ref[row])
-    if not layer:
-        w_copies[1].wait()
     key_new = rms_scale(jnp.dot(normed, wk[...], preferred_element_type=F32), kgain_ref[row])
-    if not layer:
-        w_copies[2].wait()
     value_new = jnp.dot(normed, wv[...], preferred_element_type=F32)
     pair = 2 * dim
     for c in range(heads // 2):
@@ -143,10 +145,12 @@
     weight = jnp.exp(logits - jnp.max(logits, axis=0, keepdims=True))
     probs = weight / jnp.sum(weight, axis=0, keepdims=True)
     expert_ids = lax.broadcasted_iota(jnp.int32, probs.shape, 0)
-    member = expert_ids == ids_ref[layer, 0:1]
-    for j in range(1, ids_ref.shape[1]):
-        member = member | (expert_ids == ids_ref[layer, j:j + 1])
-    gate_out[...] = jnp.where(member, probs, 0.0)
+    ids = ids_ref[layer]
+    picked = jnp.concatenate([jnp.sum(jnp.where(expert_ids == ids[j:j + 1], probs, 0.0), axis=0, keepdims=True) for j in range(ids.shape[0])], axis=0)
+    ids = ids.astype(F32)
+    low = lax.broadcasted_iota(jnp.int32, ids.shape, 1) < rows // 2
+    gate_out[0] = jnp.where(low, picked, pltpu.roll(ids, rows // 2, 1))
+    gate_out[1] = jnp.where(low, pltpu.roll(picked, rows // 2, 1), ids)
     if layer:
         for copy in first_out:
             copy.wait()
@@ -155,53 +159,32 @@
                 copy.wait()
 
 
-def attention_call(layer, x, pos, freq, ids, again, qgain, kgain, mgain, wr, kc, vc, wq, wk, wv, wo, ready):
-    layers, slots, heads, dim, rows = kc.shape
-    hidden = x.shape[1]
-    experts = wr.shape[1]
-    q_width, kv_width = wq.shape[2], wk.shape[2]
+def attention_call(small, keys, values, ready):
+    rows, hidden = small[0].shape
+    _, slots, heads, dim, _ = keys.shape
+    gate_shape = (2, small[7].shape[1], rows)
     vmem, hbm = pl.BlockSpec(memory_space=pltpu.VMEM), pl.BlockSpec(memory_space=pltpu.HBM)
-    small = (x, again, pos, freq, qgain, kgain, mgain, ids, wr)
-    out_shape = [
-        jax.ShapeDtypeStruct((rows, hidden), BF16),
-        jax.ShapeDtypeStruct((rows, hidden), BF16),
-        jax.ShapeDtypeStruct((experts, rows), F32),
-    ]
+    dma = pltpu.SemaphoreType.DMA
+    args = tuple(pltpu.with_memory_space_constraint(a, pltpu.VMEM) for a in small[:1]) + small[1:] + tuple(pltpu.with_memory_space_constraint(a, pltpu.VMEM) for a in ready)
     cache = pltpu.VMEM((heads, slots, dim, rows), BF16)
-    dma = pltpu.SemaphoreType.DMA
-    scratch = [
-        pltpu.VMEM((rows, q_width), F32),
-        pltpu.VMEM((heads, dim, rows), BF16),
-        pltpu.VMEM((heads, dim, rows), BF16),
-        pltpu.VMEM((rows, q_width), BF16),
-        pltpu.VMEM((dim // 2, rows), F32),
-        pltpu.VMEM((dim // 2, rows), F32),
-        pltpu.VMEM((2, slots, rows), F32),
-    ]
-    if layer:
-        args = small + tuple(pltpu.with_memory_space_constraint(a, pltpu.VMEM) for a in ready)
-        in_specs = [vmem] * len(args)
-        out_shape += [jax.ShapeDtypeStruct(kc.shape, kc.dtype), jax.ShapeDtypeStruct(vc.shape, vc.dtype)]
-        out_specs = [vmem] * 3 + [hbm] * 2
-        scratch = [cache, cache] + scratch + [dma((2, heads)), dma((2, heads))]
-    else:
-        args = tuple(pltpu.with_memory_space_constraint(a, pltpu.HBM) for a in small) + (kc, vc, wq, wk, wv, wo)
-        in_specs = [hbm] * len(args)
-        out_shape += [cache, cache]
-        out_specs = [vmem] * 5
-        scratch = [pltpu.VMEM(w.shape[1:], BF16) for w in (wq, wk, wv, wo)] + scratch + [dma((4,)), dma((2, heads))] + [pltpu.VMEM(a.shape, a.dtype) for a in small] + [dma((len(small),))]
     return pl.pallas_call(
-        functools.partial(attention_kernel, layer),
-        name=f"attention_{layer}",
-        out_shape=out_shape,
-        in_specs=in_specs,
-        out_specs=out_specs,
-        scratch_shapes=scratch,
+        functools.partial(attention_kernel, 1),
+        name="attention_1",
+        out_shape=[
+            jax.ShapeDtypeStruct((rows, hidden), BF16),
+            jax.ShapeDtypeStruct((rows, hidden), BF16),
+            jax.ShapeDtypeStruct(gate_shape, F32),
+            jax.ShapeDtypeStruct(keys.shape, keys.dtype),
+            jax.ShapeDtypeStruct(values.shape, values.dtype),
+        ],
+        in_specs=[vmem] * len(args),
+        out_specs=[vmem] * 3 + [hbm] * 2,
+        scratch_shapes=[cache, cache] + attention_scratch(rows, ready[2].shape[1], heads, dim, slots) + [dma((2, heads)), dma((2, heads))],
         compiler_params=pltpu.CompilerParams(vmem_limit_bytes=ATTENTION_VMEM),
     )(*args)
 
 
-def moe_kernel(layer, n_ahead, u_ref, gate_ref, x_ref, wg_hbm, wu_hbm, wd_hbm, *rest):
+def moe_kernel(layer, n_ahead, u_ref, gate_ref, x_ref, wg_hbm, wu_hbm, wd_hbm, *rest, first=None):
     ahead_hbm, out_ref, ahead, rest = rest[:n_ahead], rest[n_ahead], rest[n_ahead + 1:2 * n_ahead + 1], rest[2 * n_ahead + 1:]
     (wg, wu, wd, ag_u, ag_g, part, psib, rs_in, w_sem, agu_send, agu_recv, sbu_send, sbu_recv, agg_send, agg_recv, sbg_send, sbg_recv, ps_send, ps_recv, rs_send, rs_recv, ahead_sem) = rest
     steps, _, rows, hidden = part.shape
@@ -220,8 +203,11 @@
     sib = chip * 2 + (1 - core)
 
     w_copies = [pltpu.make_async_copy(src.at[layer], dst, w_sem.at[i]) for i, (src, dst) in enumerate(((wg_hbm, wg), (wu_hbm, wu), (wd_hbm, wd)))]
-    for copy in w_copies:
-        copy.start()
+
+    def load_experts():
+        for copy in w_copies:
+            copy.start()
+
     barrier = pltpu.get_barrier_semaphore()
     for peer in (prv, sib):
         pl.semaphore_signal(barrier, inc=1, device_id={"ep": peer}, device_id_type=MESH)
@@ -256,10 +242,15 @@
         span = pl.ds(s * rs_rows, rs_rows)
         return remote(part.at[k, 0, span], rs_in.at[k, span], rs_send.at[k, s], rs_recv.at[k, s], nxt)
 
+    if first is None:
+        load_experts()
+    else:
+        first(load_experts)
     pl.semaphore_wait(barrier, 2)
     ring_g(0, gate_ref).start()
-    for s in range(AG_SUBS):
-        ring_u(0, s, u_ref).start()
+    for turn in range(4):
+        for s in turns(AG_SUBS, turn):
+            ring_u(0, s, u_ref).start()
     sib_g(0, gate_ref).start()
     for s in range(AG_SUBS):
         sib_u(0, s, u_ref).start()
@@ -293,7 +284,7 @@
         part[k, 0, span] = total
         ring_part(k, s).start()
 
-    lane = lax.broadcasted_iota(jnp.int32, (rows, gate_ref.shape[0]), 1)
+    low = lax.broadcasted_iota(jnp.int32, (1, rows), 1) < rows // 2
     for copy in w_copies:
         copy.wait()
     ahead_copies = []
@@ -306,31 +297,43 @@
         copy.start()
 
     def one_step(k, carry):
-        def forward(s):
+        def forward(turn):
             @pl.when(k < steps - 1)
             def _():
-                take_sub(k + 1, s)
-
-        def reduce(s):
+                for s in turns(AG_SUBS, turn):
+                    take_sub(k + 1, s)
+
+        def reduce(turn):
             @pl.when(k == 2)
             def _():
-                add_sub(k - 1, s, True)
+                for s in turns(RS_SUBS, turn):
+                    add_sub(k - 1, s, True)
 
             @pl.when(k > 2)
             def _():
-                add_sub(k - 1, s, False)
+                for s in turns(RS_SUBS, turn):
+                    add_sub(k - 1, s, False)
 
         forward(0)
         sib_g(k).wait_recv()
         for s in range(AG_SUBS):
             sib_u(k, s).wait_recv()
         block = ag_u[k].reshape(2 * rows, hidden)
-        gates = [ag_g[k, j].T for j in range(2)]
+        weights = []
+        for e in range(2):
+            for j in range(2):
+                halves = []
+                for h in range(2):
+                    table = ag_g[k, j, h]
+                    wanted = pltpu.roll(table, rows // 2, 1) == (2 * me + e).astype(F32)
+                    halves.append(jnp.sum(jnp.where(wanted, table, 0.0), axis=0, keepdims=True))
+                weights.append(jnp.where(low, halves[0], pltpu.roll(halves[1], rows // 2, 1)))
+        columns = jnp.concatenate(weights + weights, axis=0).T
 
         for e in range(2):
             gate_part = jnp.dot(block, wg[e], preferred_element_type=F32)
             up_part = jnp.dot(block, wu[e], preferred_element_type=F32)
-            weight = jnp.concatenate([jnp.sum(jnp.where(lane == 2 * me + e, g, 0.0), axis=1, keepdims=True) for g in gates], axis=0)
+            weight = jnp.concatenate([columns[:, 2 * e + j:2 * e + j + 1] for j in range(2)], axis=0)
             activated = jnp.where(weight != 0.0, jax.nn.silu(gate_part) * up_part, 0.0).astype(BF16)
             forward(2 * e + 1)
             reduce(2 * e)
@@ -348,9 +351,10 @@
         return carry
 
     lax.fori_loop(0, steps, one_step, 0)
-    for s in range(RS_SUBS):
-        add_sub(steps - 1, s, False)
-    for s in range(RS_SUBS):
+    for turn in range(4):
+        for s in turns(RS_SUBS, turn):
+            add_sub(steps - 1, s, False)
+    for s in [s for turn in range(4) for s in turns(RS_SUBS, turn)]:
         span = pl.ds(s * rs_rows, rs_rows)
         sib_part(0, s).wait_recv()
         own = part[0, 0, span] + psib[0, span]
@@ -379,36 +383,84 @@
         copy.wait()
 
 
-def moe_call(layer, u, gate, x, wg, wu, wd, steps, ahead):
+def first_kernel(n_small, n_big, n_experts, n_out, n_attention, *refs):
+    it = iter(refs)
+    small, big, experts, outs, scratch, state = ([next(it) for _ in range(n)] for n in (n_small, n_big, n_experts, n_out, n_attention, 3))
+    out_ref, kbuf, vbuf, *ahead = outs
+    x_ref, u_ref, gate_ref = state
+
+    def first(loading):
+        attention_kernel(0, *small, *big, x_ref, u_ref, gate_ref, kbuf, vbuf, *ahead[2:], *scratch, loading=loading)
+
+    moe_kernel(0, n_big, u_ref, gate_ref, x_ref, *experts, *big, out_ref, *ahead, *it, first=first)
+
+
+def attention_scratch(rows, q_width, heads, dim, slots):
+    return [
+        pltpu.VMEM((rows, q_width), F32),
+        pltpu.VMEM((heads, dim, rows), BF16),
+        pltpu.VMEM((heads, dim, rows), BF16),
+        pltpu.VMEM((rows, q_width), BF16),
+        pltpu.VMEM((dim // 2, rows), F32),
+        pltpu.VMEM((dim // 2, rows), F32),
+        pltpu.VMEM((2, slots, rows), F32),
+    ]
+
+
+def moe_scratch(rows, hidden, width, gate_shape, steps, n_heads):
+    dma = pltpu.SemaphoreType.DMA
+    return [
+        pltpu.VMEM((2, hidden, width), BF16),
+        pltpu.VMEM((2, hidden, width), BF16),
+        pltpu.VMEM((2, width, hidden), BF16),
+        pltpu.VMEM((steps, 2, rows, hidden), BF16),
+        pltpu.VMEM((steps, 2) + gate_shape, F32),
+        pltpu.VMEM((steps, 2, rows, hidden), F32),
+        pltpu.VMEM((steps, rows, hidden), F32),
+        pltpu.VMEM((steps, rows, hidden), F32),
+        dma((3,)),
+        dma((steps, AG_SUBS)), dma((steps, AG_SUBS)), dma((steps, AG_SUBS)), dma((steps, AG_SUBS)),
+        dma((steps,)), dma((steps,)), dma((steps,)), dma((steps,)),
+        dma((steps, RS_SUBS)), dma((steps, RS_SUBS)), dma((steps, RS_SUBS)), dma((steps, RS_SUBS)),
+        dma((6, n_heads)),
+    ]
+
+
+def first_call(small, big, experts, steps):
+    rows, hidden = small[0].shape
+    keys, w_query = big[0], big[2]
+    _, slots, heads, dim, _ = keys.shape
+    gate_shape = (2, small[7].shape[1], rows)
+    hbm, vmem = pl.BlockSpec(memory_space=pltpu.HBM), pl.BlockSpec(memory_space=pltpu.VMEM)
+    dma = pltpu.SemaphoreType.DMA
+    cache = pltpu.VMEM((heads, slots, dim, rows), BF16)
+    out_shape = [pltpu.VMEM((rows, hidden), BF16)] + [cache] * 4 + [pltpu.VMEM(w.shape[1:], BF16) for w in big[2:]]
+    scratch = attention_scratch(rows, w_query.shape[2], heads, dim, slots) + [dma((4,)), dma((2, heads))] + [pltpu.VMEM(a.shape, a.dtype) for a in small] + [dma((len(small),))]
+    state = [pltpu.VMEM((rows, hidden), BF16), pltpu.VMEM((rows, hidden), BF16), pltpu.VMEM(gate_shape, F32)]
+    args = tuple(pltpu.with_memory_space_constraint(a, pltpu.HBM) for a in small) + big + experts
+    return pl.pallas_call(
+        functools.partial(first_kernel, len(small), len(big), len(experts), len(out_shape), len(scratch)),
+        name="attention_moe_0",
+        out_shape=out_shape,
+        in_specs=[hbm] * len(args),
+        out_specs=[vmem] * len(out_shape),
+        scratch_shapes=scratch + state + moe_scratch(rows, hidden, experts[0].shape[3], gate_shape, steps, heads),
+        compiler_params=pltpu.CompilerParams(vmem_limit_bytes=FIRST_VMEM, collective_id=0, has_side_effects=True),
+    )(*args)
+
+
+def moe_call(u, gate, x, wg, wu, wd, steps, heads):
     rows, hidden = u.shape
-    experts = gate.shape[0]
-    width = wg.shape[3]
     vmem, hbm = pl.BlockSpec(memory_space=pltpu.VMEM), pl.BlockSpec(memory_space=pltpu.HBM)
-    dma = pltpu.SemaphoreType.DMA
-    kept = [a.shape[1:] if a.ndim == 3 else (a.shape[2], a.shape[1]) + a.shape[3:] for a in ahead]
     return pl.pallas_call(
-        functools.partial(moe_kernel, layer, len(ahead)),
-        name=f"moe_{layer}",
-        out_shape=[jax.ShapeDtypeStruct((rows, hidden), BF16)] + [pltpu.VMEM(shape, BF16) for shape in kept],
-        in_specs=[vmem] * 3 + [hbm] * (3 + len(ahead)),
-        out_specs=[vmem] * (1 + len(ahead)),
-        scratch_shapes=[
-            pltpu.VMEM((2, hidden, width), BF16),
-            pltpu.VMEM((2, hidden, width), BF16),
-            pltpu.VMEM((2, width, hidden), BF16),
-            pltpu.VMEM((steps, 2, rows, hidden), BF16),
-            pltpu.VMEM((steps, 2, experts, rows), F32),
-            pltpu.VMEM((steps, 2, rows, hidden), F32),
-            pltpu.VMEM((steps, rows, hidden), F32),
-            pltpu.VMEM((steps, rows, hidden), F32),
-            dma((3,)),
-            dma((steps, AG_SUBS)), dma((steps, AG_SUBS)), dma((steps, AG_SUBS)), dma((steps, AG_SUBS)),
-            dma((steps,)), dma((steps,)), dma((steps,)), dma((steps,)),
-            dma((steps, RS_SUBS)), dma((steps, RS_SUBS)), dma((steps, RS_SUBS)), dma((steps, RS_SUBS)),
-            dma((6, 8)),
-        ],
-        compiler_params=pltpu.CompilerParams(vmem_limit_bytes=MOE_VMEM, collective_id=layer, has_side_effects=True),
-    )(u, gate, x, wg, wu, wd, *ahead)
+        functools.partial(moe_kernel, 1, 0),
+        name="moe_1",
+        out_shape=jax.ShapeDtypeStruct((rows, hidden), BF16),
+        in_specs=[vmem] * 3 + [hbm] * 3,
+        out_specs=vmem,
+        scratch_shapes=moe_scratch(rows, hidden, wg.shape[3], gate.shape, steps, heads),
+        compiler_params=pltpu.CompilerParams(vmem_limit_bytes=MOE_VMEM, collective_id=1, has_side_effects=True),
+    )(u, gate, x, wg, wu, wd)
 
 
 def solution(mesh):
@@ -425,13 +477,12 @@
         ids = jnp.transpose(expert_ids, (0, 2, 1))
         router = jnp.transpose(w_router, (0, 2, 1))
         pos = positions[None, :]
-        small = (pos, freq, ids, attn_gain, q_gain, k_gain, moe_gain, router)
+        small = (attn_gain, pos, freq, q_gain, k_gain, moe_gain, ids, router)
         big = tuple(pltpu.with_memory_space_constraint(a, pltpu.HBM) for a in (keys, values, w_query, w_key, w_value, w_out))
-        experts = tuple(pltpu.with_memory_space_constraint(a, pltpu.HBM) for a in (w_gate, w_up, w_down)) + (group_size // 2,)
-        hidden_x, u, gate, *first = attention_call(0, hidden_state, *small, *big, ())
-        hidden_x, *ready = moe_call(0, u, gate, hidden_x, *experts, big)
-        hidden_x, u, gate, *prev = attention_call(1, hidden_x, *small, *big, (*ready, *first))
-        hidden_x, = moe_call(1, u, gate, hidden_x, *experts, ())
+        experts = tuple(pltpu.with_memory_space_constraint(a, pltpu.HBM) for a in (w_gate, w_up, w_down))
+        hidden_x, k_first, v_first, *ready = first_call((hidden_state,) + small, big, experts, group_size // 2)
+        hidden_x, u, gate, *prev = attention_call((hidden_x,) + small, keys, values, (*ready, k_first, v_first))
+        hidden_x = moe_call(u, gate, hidden_x, *experts, group_size // 2, key_cache.shape[3])
         return hidden_x, jnp.transpose(prev[0], (0, 4, 1, 2, 3)), jnp.transpose(prev[1], (0, 4, 1, 2, 3))
 
     cache_spec = P(None, seq_axes, None, None, None)

time: 163 us -> 158 us (0.969)
  Pallas kernels: 161 us -> 157 us
    pallas_call x4 -> x3, Pallas kernels: 161 us -> 157 us  [the longest x1 81.1 us: first_call(): pl.pallas_call(functools.partial(first_kernel, len(small), len(big), len(...]
where the time goes in v3:
time: 158 us
  Pallas kernels  157 us (99%)
    pallas_call x1, Pallas kernels, first_call(): pl.pallas_call(functools.partial(first_kernel, len(small), len(big), len(...  81.1 us
    pallas_call x1, Pallas kernels, moe_call(): pl.pallas_call(functools.partial(moe_kernel, 1, 0), name='moe_1', out_sha...  66.8 us
    pallas_call x1, Pallas kernels, attention_call(): pl.pallas_call(functools.partial(attention_kernel, 1), name='attention_1'...  8.63 us

profile of v3, /device:TPU:0, one launch (start us, length us, event | category | flops | bytes accessed | tf_op | source)
XLA Modules:
  0.0 158.0 jit_solution(7250075642856362316)
XLA Ops:
  0.6 0.0 copy-start
  0.6 0.0 copy-start.1
  0.7 0.0 copy-start.2
  0.7 0.0 copy-start.3
  0.7 0.0 copy-start.4
  0.7 0.0 copy-start.5
  0.7 0.0 copy-start.6
  0.7 0.0 copy-start.7
  0.7 81.1 %attention_moe_0.1 = (bf16[128,1024]{1,0:T(8,128)(2,1)S(1)}, bf16[8,32,64,128]{3,2,1,0:T(8,128)(2,1)S(1)}, bf16[8,32,64,128]{3,2,1,0:T(8,128)(2,1)S(1)}, bf16[8,...) custom-call(bf16[128,1024]{1,0:T(8,128)(2,1)} %refs_0_.1, ...), custom_call_target="tpu_custom_call" | custom-call | tf_op jit(solution)/shard_map/attention_moe_0/pallas_call | solution.py:441
  81.8 0.0 copy-done
  81.8 0.0 copy-done.1
  81.8 0.0 copy-done.2
  81.8 0.0 copy-done.3
  81.8 0.0 copy-done.4
  81.8 0.0 copy-done.5
  81.9 0.0 copy-done.6
  81.9 0.0 copy-done.7
  81.9 8.6 %attention_1.1 = (bf16[128,1024]{1,0:T(8,128)(2,1)S(1)}, bf16[128,1024]{1,0:T(8,128)(2,1)S(1)}, f32[2,8,128]{2,1,0:T(8,128)S(1)}, bf16[2,32,8,64,128]{4,3,2,1,0:T(8,128)(2,1)}, bf16[2,32,8,64,128]{4,3,2,1,0:T(8,128)(2,1)}) custom-call(bf16[128,1024]{1,0:T(8,128)(2,1)S(1)} %get-tuple-element.17.rest_0_, f32[2,1024]{1,0:T(2,128)S(1)} %copy-done.2, ...), custom_call_target="tpu_custom_call" | custom-call | tf_op jit(solution)/shard_map/attention_1/pallas_call | solution.py:170
  90.5 66.8 %moe_1.1 = bf16[128,1024]{1,0:T(8,128)(2,1)S(1)} custom-call(bf16[128,1024]{1,0:T(8,128)(2,1)S(1)} %get-tuple-element.26.u_ref, f32[2,8,128]{2,1,0:T(8,128)S(1)} %get-tuple-element.27.gate_ref, bf16[128,1024]{1,0:T(8,128)(2,1)S(1)} %get-tuple-element.28.x_ref, bf16[2,2,1024,512]{3,2,1,0:T(8,128)(2,1)} %wg_hbm.1, bf16[2,2,1024,512]{3,2,1,0:T(8,128)(2,1)} %wu_hbm.1, ...), custom_call_target="tpu_custom_call" | custom-call | tf_op jit(solution)/shard_map/moe_1/pallas_call | solution.py:455
  157.3 0.7 copy.22
Async XLA Ops:
  0.6 81.2 %copy-start = (bf16[2,1024,32]{1,2,0:T(8,128)(2,1)S(1)}, bf16[2,1024,32]{1,2,0:T(8,128)(2,1)}, u32[]{:S(2)}) copy-start(bf16[2,1024,32]{1,2,0:T(8,128)(2,1)} %param.31) | copy-start | bytes 393220
  0.6 81.2 %copy-start.1 = (f32[32,128]{1,0:T(8,128)S(1)}, f32[32,128]{1,0:T(8,128)}, u32[]{:S(2)}) copy-start(f32[32,128]{1,0:T(8,128)} %constant.2.clone.refs_3_.rest_3_) | copy-start | bytes 49156
  0.7 81.2 %copy-start.2 = (f32[2,1024]{1,0:T(2,128)S(1)}, f32[2,1024]{1,0:T(2,128)}, u32[]{:S(2)}) copy-start(f32[2,1024]{1,0:T(2,128)} %rest_1_.1) | copy-start | bytes 24580
  0.7 81.2 %copy-start.3 = (f32[2,1024]{1,0:T(2,128)S(1)}, f32[2,1024]{1,0:T(2,128)}, u32[]{:S(2)}) copy-start(f32[2,1024]{1,0:T(2,128)} %rest_4_.1) | copy-start | bytes 24580
  0.7 81.2 %copy-start.4 = (f32[2,1024]{1,0:T(2,128)S(1)}, f32[2,1024]{1,0:T(2,128)}, u32[]{:S(2)}) copy-start(f32[2,1024]{1,0:T(2,128)} %rest_6_.1) | copy-start | bytes 24580
  0.7 81.2 %copy-start.5 = (s32[2,128,8]{1,2,0:T(8,128)S(1)}, s32[2,128,8]{1,2,0:T(8,128)}, u32[]{:S(2)}) copy-start(s32[2,128,8]{1,2,0:T(8,128)} %param.22) | copy-start | bytes 24580
  0.7 81.2 %copy-start.6 = (f32[2,512]{1,0:T(2,128)S(1)}, f32[2,512]{1,0:T(2,128)}, u32[]{:S(2)}) copy-start(f32[2,512]{1,0:T(2,128)} %rest_5_.1) | copy-start | bytes 12292
  0.7 81.2 %copy-start.7 = (s32[128]{0:T(128)S(1)}, s32[128]{0:T(128)}, u32[]{:S(2)}) copy-start(s32[128]{0:T(128)} %param.21) | copy-start | bytes 1540

commit v4 on v3

--- a/solution.py
+++ b/solution.py
@@ -27,6 +27,10 @@
 def rms_scale(tensor, gain):
     mean_sq = jnp.mean(tensor * tensor, axis=-1, keepdims=True)
     return tensor * lax.rsqrt(mean_sq + NORM_EPS) * gain
+
+
+def spread_positions(pos, dim):
+    return jnp.broadcast_to(pos.astype(F32), (dim, pos.shape[1])).astype(BF16)
 
 
 def attention_kernel(layer, *rest, loading=None):
@@ -95,8 +99,9 @@
         for j in range(2):
             v_t[2 * c + j] = chunk[j * dim:(j + 1) * dim]
 
-    pos_b = jnp.broadcast_to(pos.astype(F32), (dim, rows)).astype(BF16)
-    slot_ids = lax.broadcasted_iota(jnp.int32, (slots, rows), 0)
+    pos_b = spread_positions(pos, dim)
+    slot_ids = lax.broadcasted_iota(jnp.int32, score.shape[1:], 0)
+    visible = slot_ids <= pos if layer else (slot_ids < pos) | (slot_ids == slots)
 
     def one_head(n, carry):
         cols = pl.ds(pl.multiple_of(n * pair, pair), pair)
@@ -108,15 +113,21 @@
         if not layer:
             k_copy.wait()
         for s in range(slots):
-            key = jnp.where(pos_b == s, k_new, k_raw[n, s])
-            kbuf[n, s] = key
+            key = k_raw[n, s]
+            if layer:
+                key = jnp.where(pos_b == s, k_new, key)
+                kbuf[n, s] = key
             key = key.astype(F32)
             score[0, s:s + 1] = jnp.sum(key * q0, axis=0, keepdims=True)
             score[1, s:s + 1] = jnp.sum(key * q1, axis=0, keepdims=True)
         if layer:
             k_copy.start()
+        else:
+            key = k_new.astype(F32)
+            score[0, slots:slots + 1] = jnp.sum(key * q0, axis=0, keepdims=True)
+            score[1, slots:slots + 1] = jnp.sum(key * q1, axis=0, keepdims=True)
         for g in range(2):
-            masked = jnp.where(slot_ids <= pos, score[g], -jnp.inf)
+            masked = jnp.where(visible, score[g], -jnp.inf)
             weight = jnp.exp(masked - jnp.max(masked, axis=0, keepdims=True))
             score[g] = (weight / jnp.sum(weight, axis=0, keepdims=True)).astype(BF16).astype(F32)
         if not layer:
@@ -124,11 +135,17 @@
         acc0 = jnp.zeros((dim, rows), F32)
         acc1 = jnp.zeros((dim, rows), F32)
         for s in range(slots):
-            value = jnp.where(pos_b == s, v_new, v_raw[n, s])
-            vbuf[n, s] = value
+            value = v_raw[n, s]
+            if layer:
+                value = jnp.where(pos_b == s, v_new, value)
+                vbuf[n, s] = value
             value = value.astype(F32)
             acc0 += value * score[0, s:s + 1]
             acc1 += value * score[1, s:s + 1]
+        if not layer:
+            value = v_new.astype(F32)
+            acc0 += value * score[0, slots:slots + 1]
+            acc1 += value * score[1, slots:slots + 1]
         if layer:
             v_copy.start()
         o_rows[:, cols] = jnp.concatenate([acc0, acc1], axis=0).T.astype(BF16)
@@ -184,7 +201,7 @@
     )(*args)
 
 
-def moe_kernel(layer, n_ahead, u_ref, gate_ref, x_ref, wg_hbm, wu_hbm, wd_hbm, *rest, first=None):
+def moe_kernel(layer, n_ahead, u_ref, gate_ref, x_ref, wg_hbm, wu_hbm, wd_hbm, *rest, first=None, idle=None):
     ahead_hbm, out_ref, ahead, rest = rest[:n_ahead], rest[n_ahead], rest[n_ahead + 1:2 * n_ahead + 1], rest[2 * n_ahead + 1:]
     (wg, wu, wd, ag_u, ag_g, part, psib, rs_in, w_sem, agu_send, agu_recv, sbu_send, sbu_recv, agg_send, agg_recv, sbg_send, sbg_recv, ps_send, ps_recv, rs_send, rs_recv, ahead_sem) = rest
     steps, _, rows, hidden = part.shape
@@ -346,8 +363,12 @@
             if e == 0:
                 forward(2)
             reduce(2 * e + 1)
+            if e == 0 and idle is not None:
+                idle(k, 0)
         for s in range(RS_SUBS):
             sib_part(k, s).start()
+        if idle is not None:
+            idle(k, 1)
         return carry
 
     lax.fori_loop(0, steps, one_step, 0)
@@ -392,10 +413,22 @@
     def first(loading):
         attention_kernel(0, *small, *big, x_ref, u_ref, gate_ref, kbuf, vbuf, *ahead[2:], *scratch, loading=loading)
 
-    moe_kernel(0, n_big, u_ref, gate_ref, x_ref, *experts, *big, out_ref, *ahead, *it, first=first)
-
-
-def attention_scratch(rows, q_width, heads, dim, slots):
+    heads, slots, dim, _ = kbuf.shape
+    k_t, v_t, pos_ref = scratch[1], scratch[2], scratch[11]
+
+    def idle(k, turn):
+        @pl.when((k >= 3) & (k < 3 + heads // 2))
+        def _():
+            n = 2 * (k - 3) + turn
+            pos_b = spread_positions(pos_ref[...], dim)
+            for s in range(slots):
+                for buf, new in ((kbuf, k_t), (vbuf, v_t)):
+                    buf[n, s] = jnp.where(pos_b == s, new[n], buf[n, s])
+
+    moe_kernel(0, n_big, u_ref, gate_ref, x_ref, *experts, *big, out_ref, *ahead, *it, first=first, idle=idle)
+
+
+def attention_scratch(rows, q_width, heads, dim, score_rows):
     return [
         pltpu.VMEM((rows, q_width), F32),
         pltpu.VMEM((heads, dim, rows), BF16),
@@ -403,7 +436,7 @@
         pltpu.VMEM((rows, q_width), BF16),
         pltpu.VMEM((dim // 2, rows), F32),
         pltpu.VMEM((dim // 2, rows), F32),
-        pltpu.VMEM((2, slots, rows), F32),
+        pltpu.VMEM((2, score_rows, rows), F32),
     ]
 
 
@@ -435,7 +468,7 @@
     dma = pltpu.SemaphoreType.DMA
     cache = pltpu.VMEM((heads, slots, dim, rows), BF16)
     out_shape = [pltpu.VMEM((rows, hidden), BF16)] + [cache] * 4 + [pltpu.VMEM(w.shape[1:], BF16) for w in big[2:]]
-    scratch = attention_scratch(rows, w_query.shape[2], heads, dim, slots) + [dma((4,)), dma((2, heads))] + [pltpu.VMEM(a.shape, a.dtype) for a in small] + [dma((len(small),))]
+    scratch = attention_scratch(rows, w_query.shape[2], heads, dim, slots + 8) + [dma((4,)), dma((2, heads))] + [pltpu.VMEM(a.shape, a.dtype) for a in small] + [dma((len(small),))]
     state = [pltpu.VMEM((rows, hidden), BF16), pltpu.VMEM((rows, hidden), BF16), pltpu.VMEM(gate_shape, F32)]
     args = tuple(pltpu.with_memory_space_constraint(a, pltpu.HBM) for a in small) + big + experts
     return pl.pallas_call(

time: 158 us -> 158 us (level)
  no operation moved by 1% of the time
where the time goes in v4:
time: 158 us
  Pallas kernels  156 us (99%)
    pallas_call x1, Pallas kernels, first_call(): pl.pallas_call(functools.partial(first_kernel, len(small), len(big), len(...  80.6 us
    pallas_call x1, Pallas kernels, moe_call(): pl.pallas_call(functools.partial(moe_kernel, 1, 0), name='moe_1', out_sha...  66.8 us
    pallas_call x1, Pallas kernels, attention_call(): pl.pallas_call(functools.partial(attention_kernel, 1), name='attention_1'...  8.64 us

profile of v4, /device:TPU:0, one launch (start us, length us, event | category | flops | bytes accessed | tf_op | source)
XLA Modules:
  0.0 157.6 jit_solution(1040044107053329077)
XLA Ops:
  0.6 0.0 copy-start
  0.6 0.0 copy-start.1
  0.7 0.0 copy-start.2
  0.7 0.0 copy-start.3
  0.7 0.0 copy-start.4
  0.7 0.0 copy-start.5
  0.7 0.0 copy-start.6
  0.7 0.0 copy-start.7
  0.7 80.6 %attention_moe_0.1 = (bf16[128,1024]{1,0:T(8,128)(2,1)S(1)}, bf16[8,32,64,128]{3,2,1,0:T(8,128)(2,1)S(1)}, bf16[8,32,64,128]{3,2,1,0:T(8,128)(2,1)S(1)}, bf16[8,...) custom-call(bf16[128,1024]{1,0:T(8,128)(2,1)} %refs_0_.1, ...), custom_call_target="tpu_custom_call" | custom-call | tf_op jit(solution)/shard_map/attention_moe_0/pallas_call | solution.py:474
  81.3 0.0 copy-done
  81.3 0.0 copy-done.1
  81.3 0.0 copy-done.2
  81.3 0.0 copy-done.3
  81.4 0.0 copy-done.4
  81.4 0.0 copy-done.5
  81.4 0.0 copy-done.6
  81.4 0.0 copy-done.7
  81.4 8.6 %attention_1.1 = (bf16[128,1024]{1,0:T(8,128)(2,1)S(1)}, bf16[128,1024]{1,0:T(8,128)(2,1)S(1)}, f32[2,8,128]{2,1,0:T(8,128)S(1)}, bf16[2,32,8,64,128]{4,3,2,1,0:T(8,128)(2,1)}, bf16[2,32,8,64,128]{4,3,2,1,0:T(8,128)(2,1)}) custom-call(bf16[128,1024]{1,0:T(8,128)(2,1)S(1)} %get-tuple-element.17.rest_0_, f32[2,1024]{1,0:T(2,128)S(1)} %copy-done.2, ...), custom_call_target="tpu_custom_call" | custom-call | tf_op jit(solution)/shard_map/attention_1/pallas_call | solution.py:187
  90.0 66.8 %moe_1.1 = bf16[128,1024]{1,0:T(8,128)(2,1)S(1)} custom-call(bf16[128,1024]{1,0:T(8,128)(2,1)S(1)} %get-tuple-element.26.u_ref, f32[2,8,128]{2,1,0:T(8,128)S(1)} %get-tuple-element.27.gate_ref, bf16[128,1024]{1,0:T(8,128)(2,1)S(1)} %get-tuple-element.28.x_ref, bf16[2,2,1024,512]{3,2,1,0:T(8,128)(2,1)} %wg_hbm.1, bf16[2,2,1024,512]{3,2,1,0:T(8,128)(2,1)} %wu_hbm.1, ...), custom_call_target="tpu_custom_call" | custom-call | tf_op jit(solution)/shard_map/moe_1/pallas_call | solution.py:488
  156.9 0.7 copy.22
Async XLA Ops:
  0.6 80.7 %copy-start = (bf16[2,1024,32]{1,2,0:T(8,128)(2,1)S(1)}, bf16[2,1024,32]{1,2,0:T(8,128)(2,1)}, u32[]{:S(2)}) copy-start(bf16[2,1024,32]{1,2,0:T(8,128)(2,1)} %param.31) | copy-start | bytes 393220
  0.6 80.7 %copy-start.1 = (f32[32,128]{1,0:T(8,128)S(1)}, f32[32,128]{1,0:T(8,128)}, u32[]{:S(2)}) copy-start(f32[32,128]{1,0:T(8,128)} %constant.2.clone.refs_3_.rest_3_) | copy-start | bytes 49156
  0.7 80.7 %copy-start.2 = (f32[2,1024]{1,0:T(2,128)S(1)}, f32[2,1024]{1,0:T(2,128)}, u32[]{:S(2)}) copy-start(f32[2,1024]{1,0:T(2,128)} %rest_1_.1) | copy-start | bytes 24580
  0.7 80.7 %copy-start.3 = (f32[2,1024]{1,0:T(2,128)S(1)}, f32[2,1024]{1,0:T(2,128)}, u32[]{:S(2)}) copy-start(f32[2,1024]{1,0:T(2,128)} %rest_4_.1) | copy-start | bytes 24580
  0.7 80.7 %copy-start.4 = (f32[2,1024]{1,0:T(2,128)S(1)}, f32[2,1024]{1,0:T(2,128)}, u32[]{:S(2)}) copy-start(f32[2,1024]{1,0:T(2,128)} %rest_6_.1) | copy-start | bytes 24580
  0.7 80.7 %copy-start.5 = (s32[2,128,8]{1,2,0:T(8,128)S(1)}, s32[2,128,8]{1,2,0:T(8,128)}, u32[]{:S(2)}) copy-start(s32[2,128,8]{1,2,0:T(8,128)} %param.22) | copy-start | bytes 24580
  0.7 80.7 %copy-start.6 = (f32[2,512]{1,0:T(2,128)S(1)}, f32[2,512]{1,0:T(2,128)}, u32[]{:S(2)}) copy-start(f32[2,512]{1,0:T(2,128)} %rest_5_.1) | copy-start | bytes 12292
  0.7 80.7 %copy-start.7 = (s32[128]{0:T(128)S(1)}, s32[128]{0:T(128)}, u32[]{:S(2)}) copy-start(s32[128]{0:T(128)} %param.21) | copy-start | bytes 1540
